TPU v7x, 256 devices: a 4x2x16 block of a 4x16x16 slice. The times are simulated.
256 devices in a mesh: tracts: 2 (over y), sky: 32 (over z, core), depth: 4 (over x).
Axes of the slice: x: 4, y: 2, z: 16, core: 2. Of those that a mesh axis runs over, the one named last changes fastest.
The devices are a block of a 4x16x16 slice.
Arguments:
- visit_tiles: bfloat16 [1024, 32, 64, 512], P(('tracts', 'sky', 'depth')), parts along dimension 0, may hold values from -6 to 6
- warp_matrix: bfloat16 [1024, 512, 512], P(('tracts', 'sky', 'depth')), parts along dimension 0, may hold values from -0.25 to 0.25
- flux_scale: float32 [1024], P(('tracts', 'sky', 'depth')), parts along dimension 0, may hold values from 0.3 to 3
- patch_lists: int32 [1024, 32], P(('tracts', 'sky', 'depth')), parts along dimension 0, may hold values from 0 to 127, all different within a row; in each aligned block of 4 rows (0 to 3, 4 to 7, ...) at most 2 rows name the same one
- clip_bits: int32 [1024, 32, 4, 512], P(('tracts', 'sky', 'depth')), parts along dimension 0, may hold values from -2147483648 to 2147483647, as said below
Outputs:
- coadd_mean: float32 [2, 256, 64, 512], P(None, ('tracts', 'sky'), 'depth'), parts along dimension 1
- coadd_var: float32 [2, 256, 64, 512], P(None, ('tracts', 'sky'), 'depth'), parts along dimension 1
There are 2 independent parts, one for each index of `tracts`. A program takes and returns all parts, laid end to end along the dimension named above; each array names one. Nothing has to cross between parts.
Inputs may be any that keep to these rules, and one draw needn't show every extreme that they name: `patch_lists`: row v names the 32 different patches of visit v's blocks. In the rows of one device no patch is named more than 2 times, a bound that some block reaches there; every patch is named by some row. Bit 16 t + j of clip_bits[v, k, g, c] is 1 when clip pass t (t = 0 or 1) keeps the sample of visit v's block k at row 16 g + j, column c.
All inputs are finite; a program needn't handle non-finite values.
Results may differ from a plain program's by a relative error of at most 0.0029.
Values may be sent and summed in bfloat16 or wider, within the bound.
No kernel may reach another device: no remote copies, remote signals or barrier semaphores. Data moves between devices by JAX's collectives and lax.ppermute only.
A program may use at most 128 MiB of HBM per device.

v0:
```python
import functools

import jax
import jax.numpy as jnp
from jax import lax
from jax.experimental import pallas as pl
from jax.experimental.pallas import tpu as pltpu
from jax.sharding import Mesh
from jax.sharding import PartitionSpec as P

PATCH_DEV = 4
CORES = 2
WORD_ROWS = 16
LANES = 128
ROWS = 8
WORDS = 8
SUMS = 5
RADIX = 4096
CHUNKS = (((0, 0),), ((1, 0), (0, 1)), ((1, 1),))


def warp_kernel(depth, chunks, where_ref, scale_ref, tiles_ref, matrix_ref, *out_refs):
    here, core = where_ref[0], where_ref[1]
    factor = scale_ref[pl.program_id(0)]
    blocks, columns = tiles_ref.shape[1], tiles_ref.shape[3]
    half = columns // CORES
    width = LANES * (1 + max(part for units in chunks for _, part in units))
    low = pl.multiple_of(core * half, half)
    high = pl.multiple_of((1 - core) * half, half)
    matrix = jnp.concatenate(
        [matrix_ref[0, :, pl.ds(low, width)], matrix_ref[0, :, pl.ds(high, width)]], axis=1
    )
    for k in range(depth):
        row = pl.multiple_of(lax.rem(here + k, depth) * WORD_ROWS, WORD_ROWS)
        rows = tiles_ref[0, :, pl.ds(row, WORD_ROWS), :].reshape(blocks * WORD_ROWS, columns)
        product = jnp.dot(rows, matrix, preferred_element_type=jnp.float32) * factor
        product = product.reshape(blocks, WORD_ROWS, CORES * width)
        for n, units in enumerate(chunks):
            for h in range(CORES):
                out = out_refs[(n * depth + k) * CORES + h]
                pieces = []
                for high_rows, part in units:
                    start = h * width + part * LANES
                    pieces.append(
                        product[:, high_rows * ROWS : (high_rows + 1) * ROWS, start : start + LANES]
                    )
                piece = pieces[0] if len(pieces) == 1 else jnp.concatenate(pieces, axis=1)
                out[...] = piece.astype(jnp.bfloat16)


def warp_some(visit_tiles, warp_matrix, flux_scale, where, depth, chunks):
    visits, blocks, rows, columns = visit_tiles.shape
    heights = [ROWS * len(units) for units in chunks for _ in range(depth * CORES)]
    return pl.pallas_call(
        functools.partial(warp_kernel, depth, chunks),
        out_shape=[
            jax.ShapeDtypeStruct((visits * blocks, height, LANES), jnp.bfloat16)
            for height in heights
        ],
        grid=(visits,),
        in_specs=[
            pl.BlockSpec(memory_space=pltpu.SMEM),
            pl.BlockSpec(memory_space=pltpu.SMEM),
            pl.BlockSpec((1, blocks, rows, columns), lambda v: (v, 0, 0, 0)),
            pl.BlockSpec((1, columns, columns), lambda v: (v, 0, 0)),
        ],
        out_specs=[pl.BlockSpec((blocks, height, LANES), lambda v: (v, 0, 0)) for height in heights],
        cost_estimate=pl.CostEstimate(
            flops=2 * visits * blocks * rows * columns * columns,
            bytes_accessed=4 * visits * blocks * rows * columns,
            transcendentals=0,
        ),
        name="warp_some",
    )(where, flux_scale, visit_tiles, warp_matrix)


def sums_kernel(units, sources, patch_ref, *refs):
    tile_refs, bit_refs, out_ref = refs[:sources], refs[sources : 2 * sources], refs[-1]
    patches = out_ref.shape[0]
    entries = tile_refs[0].shape[0]
    group = 4
    positions = lax.broadcasted_iota(jnp.int32, (ROWS, LANES), 0)
    first_masks, second_masks = [], []
    for high_rows, _ in units:
        first_masks.append(lax.shift_left(jnp.ones_like(positions), positions + high_rows * ROWS))
        second_masks.append(lax.shift_left(first_masks[-1], jnp.full_like(positions, WORD_ROWS)))

    def clear(p, _):
        out_ref[p] = jnp.zeros(out_ref.shape[1:], jnp.float32)
        return 0

    lax.fori_loop(0, patches, clear, 0)
    for s in range(sources):

        def step(g, _, s=s):
            base = pl.multiple_of(g * WORDS, WORDS)
            words = [
                bit_refs[s][pl.ds(base, WORDS), pl.ds(part * LANES, LANES)] for _, part in units
            ]
            for j in range(0, WORDS, group):
                ids = [patch_ref[s, base + j + i] for i in range(group)]
                held = [out_ref[p] for p in ids]
                for i in range(group):
                    block = tile_refs[s][base + j + i].astype(jnp.float32)
                    for n, (high_rows, _) in enumerate(units):
                        rows = slice(n * ROWS, (n + 1) * ROWS)
                        samples = block[rows]
                        word = jnp.broadcast_to(words[n][j + i : j + i + 1], (ROWS, LANES))
                        one = lax.bitwise_and(word, first_masks[n]) != 0
                        two = one & (lax.bitwise_and(word, second_masks[n]) != 0)
                        counts = jnp.where(two, 1.0 + RADIX, jnp.where(one, 1.0, 0.0))
                        square = samples * samples
                        old = held[i][:, rows]
                        out_ref[ids[i], 0, rows] = old[0] + counts
                        out_ref[ids[i], 1, rows] = old[1] + jnp.where(one, samples, 0.0)
                        out_ref[ids[i], 2, rows] = old[2] + jnp.where(one, square, 0.0)
                        out_ref[ids[i], 3, rows] = old[3] + jnp.where(two, samples, 0.0)
                        out_ref[ids[i], 4, rows] = old[4] + jnp.where(two, square, 0.0)
            return 0

        lax.fori_loop(0, entries // WORDS, step, 0)


def sums_part(tiles, bits, patch_ids, patches, units):
    sources, entries, height = len(tiles), tiles[0].shape[0], ROWS * len(units)
    return pl.pallas_call(
        functools.partial(sums_kernel, units, sources),
        out_shape=jax.ShapeDtypeStruct((patches, SUMS, height, LANES), jnp.float32),
        in_specs=[pl.BlockSpec(memory_space=pltpu.SMEM)]
        + [pl.BlockSpec(memory_space=pltpu.VMEM)] * (2 * sources),
        out_specs=pl.BlockSpec(memory_space=pltpu.VMEM),
        cost_estimate=pl.CostEstimate(
            flops=50 * sources * entries * height * LANES,
            bytes_accessed=4 * patches * SUMS * height * LANES,
            transcendentals=0,
        ),
        name="sums_part",
    )(patch_ids, *tiles, *bits)


def chain(sums):
    chips, here, own = lax.axis_size("chip"), lax.axis_index("chip"), PATCH_DEV * CORES

    def local(offset):
        return lax.dynamic_slice_in_dim(sums, lax.rem(here + offset + chips, chips) * own, own, 0)

    def send(value, sign):
        return lax.ppermute(value, "chip", [(i, (i + sign) % chips) for i in range(chips)])

    up = send(local(chips // 2), 1)

    def step(i, came):
        reach = chips // 2 - i
        return send(local(reach) + came[0], 1), send(local(-reach) + came[1], -1)

    up, down = lax.fori_loop(1, chips // 2, step, (up, jnp.zeros_like(up)))
    return local(0) + up + down


def finish(sums):
    packed, sum_first, square_first, sum_both, square_both = (sums[:, i] for i in range(SUMS))
    count_both = jnp.floor(packed * (1.0 / RADIX))
    count_first = packed - count_both * RADIX
    first_mean = sum_first / jnp.maximum(count_first, 1.0)
    first_var = (square_first - sum_first * first_mean) / jnp.maximum(count_first - 1.0, 1.0)
    some = jnp.maximum(count_both, 1.0)
    shift_sum = sum_both - count_both * first_mean
    final_mean = first_mean + shift_sum / some
    final_var = (square_both - sum_both * (sum_both / some)) / jnp.maximum(count_both - 1.0, 1.0)
    return jnp.stack([first_mean, final_mean, first_var, final_var])


def per_device(visit_tiles, warp_matrix, flux_scale, patch_lists, clip_bits):
    visits, blocks, _, columns = visit_tiles.shape
    entries = visits * blocks
    chips, depth = lax.axis_size("chip"), lax.axis_size("depth")
    patches = PATCH_DEV * CORES * chips
    half = columns // CORES
    here, core = lax.axis_index("depth"), lax.axis_index("core")
    where = jnp.stack([here, core]).astype(jnp.int32)

    def place(d, c):
        return c * depth + d

    def send(value, k, h):
        if k == 0 and h == 0:
            return value
        pairs = [
            (place(d, c), place((d + k) % depth, c ^ h)) for c in range(CORES) for d in range(depth)
        ]
        return lax.ppermute(value, ("core", "depth"), pairs)

    words = clip_bits.reshape(entries, depth, CORES, half).transpose(1, 2, 0, 3)
    names = jnp.zeros((8, half), jnp.int32).at[0, :entries].set(patch_lists.reshape(entries))
    bits = []
    for k in range(depth):
        for h in range(CORES):
            message = words[lax.rem(here + k, depth), core if h == 0 else 1 - core]
            bits.append(jnp.concatenate([message, names]))
    where, bits = lax.optimization_barrier((where, bits))
    bits = [send(bits[k * CORES + h], k, h) for k in range(depth) for h in range(CORES)]
    patch_ids = jnp.stack([b[entries, :entries] for b in bits])

    pieces = []
    for chunks in (CHUNKS[:1], CHUNKS[1:]):
        pieces += warp_some(visit_tiles, warp_matrix, flux_scale, where, depth, chunks)
    sources = depth * CORES
    tiles = []
    for n in range(len(CHUNKS)):
        mine = pieces[n * sources : (n + 1) * sources]
        tiles.append([send(mine[k * CORES + h], k, h) for k in range(depth) for h in range(CORES)])
    totals = []
    for n, units in enumerate(CHUNKS):
        sums = sums_part(tiles[n], bits, patch_ids, patches, units)
        if n + 1 < len(CHUNKS):
            rows = lax.optimization_barrier(sums.reshape(-1, LANES))
            rows = lax.psum_scatter(rows, "chip", scatter_dimension=0, tiled=True)
            rows = lax.optimization_barrier(rows)
            totals.append(rows.reshape(-1, *sums.shape[1:]))
        else:
            totals.append(chain(sums))
    squares = {}
    for total, units in zip(totals, CHUNKS):
        results = finish(total)
        for n, unit in enumerate(units):
            squares[unit] = results[:, :, n * ROWS : (n + 1) * ROWS]
    results = jnp.concatenate(
        [
            jnp.concatenate([squares[r, q] for q in range(half // LANES)], axis=-1)
            for r in range(WORD_ROWS // ROWS)
        ],
        axis=-2,
    ).reshape(4, CORES, PATCH_DEV, WORD_ROWS, half)
    own, other = results[:, core], results[:, 1 - core]
    other = lax.ppermute(other, "core", [(c, c ^ 1) for c in range(CORES)])
    low, high = jnp.where(core == 0, own, other), jnp.where(core == 0, other, own)
    joined = jnp.concatenate([low, high], axis=-1)
    return joined[:2], joined[2:]


def solution(mesh):
    tracts, sky, depth = mesh.devices.shape
    fine = Mesh(
        mesh.devices.reshape(tracts, sky // CORES, CORES, depth),
        ("tracts", "chip", "core", "depth"),
    )
    every = ("tracts", "chip", "core", "depth")
    placed = (
        P(every, None, None, None),
        P(every, None, None),
        P(every),
        P(every, None),
        P(every, None, None, None),
    )
    out = P(None, ("tracts", "chip", "core"), "depth", None)

    return jax.shard_map(
        per_device, mesh=fine, in_specs=placed, out_specs=(out, out), check_vma=False
    )
```

profile of v0, /device:TPU:33, one launch (start us, length us, event | category | flops | bytes accessed | tf_op | source)
XLA Modules:
  0.0 290.4 jit_solution(13359846169290317500)
XLA Ops:
  8.0 2.1 reshape.527
  10.8 0.9 constant_dynamic-slice_fusion.1
  11.9 20.5 %collective-permute-start.2 = (s32[136,256]{1,0:T(8,128)S(1)}, s32[136,256]{1,0:T(8,128)S(1)}, u32[]{:S(2)}, u32[]{:S(2)}) collective-permute-start(s32[136,256]{1,0:T(8,128)S(1)} %get-tuple-element.143), channel_id=1, source_target_pairs={{0,4},{1,5},{2,6},{3,7},{4,0},{5,1},{6,2},{7,3},{8,12},{9,13},{10,... | collective-permute-start | bytes 417800 | tf_op jit(solution)/shard_map/ppermute | solution.py:191
  32.5 4.2 %collective-permute-start.5 = (s32[136,256]{1,0:T(8,128)S(1)}, s32[136,256]{1,0:T(8,128)S(1)}, u32[]{:S(2)}, u32[]{:S(2)}) collective-permute-start(s32[136,256]{1,0:T(8,128)S(1)} %get-tuple-element.146), channel_id=1, source_target_pairs={{0,2},{1,3},{2,0},{3,1},{4,6},{5,7},{6,4},{7,5},{8,10},{9,11},{10,... | collective-permute-start | bytes 417800 | tf_op jit(solution)/shard_map/ppermute | solution.py:191
  36.6 6.7 %warp_some.2 = (bf16[128,8,128]{2,1,0:T(8,128)(2,1)}, bf16[128,8,128]{2,1,0:T(8,128)(2,1)}, bf16[128,8,128]{2,1,0:T(8,128)(2,1)}, bf16[128,8,128]{2,1,0:T(8,128)...) custom-call(s32[2]{0:T(128)} %pad_add_fusion.8.where_ref, ...), custom_call_target="tpu_custom_call" | custom-call | flops 4294967296 | bytes 16777216 | tf_op jit(solution)/shard_map/warp_some/pallas_call | solution.py:54
  44.0 1.0 collective-permute-done.4.refs_11_
  45.1 1.6 collective-permute-start.7
  46.7 1.1 collective-permute-start.8
  47.8 5.7 %collective-permute-done.6.refs_13_ = s32[136,256]{1,0:T(8,128)S(1)} collective-permute-done((s32[136,256]{1,0:T(8,128)S(1)}, s32[136,256]{1,0:T(8,128)S(1)}, u32[]{:S(2)}, u32[]{:S(2)}) %collective-permute-start.6) | collective-permute-done | bytes 139296 | tf_op jit(solution)/shard_map/ppermute | solution.py:191
  53.5 0.9 collective-permute-done.7.refs_14_
  54.4 2.3 collective-permute-start.12
  56.7 0.9 collective-permute-done.8.refs_15_
  57.7 0.8 collective-permute-start.13
  58.5 2.2 collective-permute-start.14
  60.7 0.8 collective-permute-start.15
  62.2 0.8 collective-permute-done.11.refs_3_
  63.0 5.8 %collective-permute-done.12.refs_4_ = bf16[128,8,128]{2,1,0:T(8,128)(2,1)S(1)} collective-permute-done((bf16[128,8,128]{2,1,0:T(8,128)(2,1)}, bf16[128,8,128]{2,1,0:T(8,128)(2,1)S(1)}, u32[]{:S(2)}, u32[]{:S(2)}) %collective-permute-start.12) | collective-permute-done | bytes 262176 | tf_op jit(solution)/shard_map/ppermute | solution.py:191
  68.8 5.8 %collective-permute-done.13.refs_5_ = bf16[128,8,128]{2,1,0:T(8,128)(2,1)S(1)} collective-permute-done((bf16[128,8,128]{2,1,0:T(8,128)(2,1)}, bf16[128,8,128]{2,1,0:T(8,128)(2,1)S(1)}, u32[]{:S(2)}, u32[]{:S(2)}) %collective-permute-start.13) | collective-permute-done | bytes 262176 | tf_op jit(solution)/shard_map/ppermute | solution.py:191
  74.6 5.8 %collective-permute-done.15.refs_7_ = bf16[128,8,128]{2,1,0:T(8,128)(2,1)S(1)} collective-permute-done((bf16[128,8,128]{2,1,0:T(8,128)(2,1)}, bf16[128,8,128]{2,1,0:T(8,128)(2,1)S(1)}, u32[]{:S(2)}, u32[]{:S(2)}) %collective-permute-start.15) | collective-permute-done | bytes 262176 | tf_op jit(solution)/shard_map/ppermute | solution.py:191
  81.1 8.5 %sums_part.3 = f32[128,5,8,128]{3,2,1,0:T(8,128)} custom-call(s32[8,128]{1,0:T(8,128)} %stack.17.patch_ref, bf16[128,8,128]{2,1,0:T(8,128)(2,1)} %get-tuple-element.151.refs_0_, bf16[128,8,128]{2,1,0:T(8,128)(2,1)} %copy-done.14, bf16[128,8,128]{2,1,0:T(8,128)(2,1)} %copy-done.15, bf16[128,8,128]{2,1,0:T(8,128)(2,1)} %copy-done.22, ...), custom_call_target="tpu_custom_call" | custom-call | flops 52428800 | bytes 2621440 | tf_op jit(solution)/shard_map/sums_part/pallas_call | solution.py:126
  89.7 8.9 %warp_some.3 = (bf16[128,16,128]{2,1,0:T(8,128)(2,1)}, bf16[128,16,128]{2,1,0:T(8,128)(2,1)}, bf16[128,16,128]{2,1,0:T(8,128)(2,1)}, bf16[128,16,128]{2,1,0:T(8,...) custom-call(s32[2]{0:T(128)} %pad_add_fusion.8.where_ref, ...), custom_call_target="tpu_custom_call" | custom-call | flops 4294967296 | bytes 16777216 | tf_op jit(solution)/shard_map/warp_some/pallas_call | solution.py:54
  98.8 3.3 %collective-permute-start.17 = (bf16[128,16,128]{2,1,0:T(8,128)(2,1)}, bf16[128,16,128]{2,1,0:T(8,128)(2,1)S(1)}, u32[]{:S(2)}, u32[]{:S(2)}) collective-permute-start(bf16[128,16,128]{2,1,0:T(8,128)(2,1)} %get-tuple-element.161), channel_id=1, source_target_pairs={{0,1},{1,2},{2,3},{3,0},{4,5},{5,6},{6,7},{7,4},{8,9},{9,10},{10,1... | collective-permute-start | bytes 1572872 | tf_op jit(solution)/shard_map/ppermute | solution.py:191
  102.5 0.8 collective-permute-start.19
  103.3 2.3 collective-permute-start.20
  105.6 2.6 collective-permute-start.21
  108.3 5.6 %collective-permute-done.17.refs_2_ = bf16[128,16,128]{2,1,0:T(8,128)(2,1)S(1)} collective-permute-done((bf16[128,16,128]{2,1,0:T(8,128)(2,1)}, bf16[128,16,128]{2,1,0:T(8,128)(2,1)S(1)}, u32[]{:S(2)}, u32[]{:S(2)}) %collective-permute-start.17) | collective-permute-done | bytes 524320 | tf_op jit(solution)/shard_map/ppermute | solution.py:191
  113.9 3.0 %collective-permute-start.22 = (bf16[128,16,128]{2,1,0:T(8,128)(2,1)}, bf16[128,16,128]{2,1,0:T(8,128)(2,1)}, u32[]{:S(2)}, u32[]{:S(2)}) collective-permute-start(bf16[128,16,128]{2,1,0:T(8,128)(2,1)} %get-tuple-element.166), channel_id=1, source_target_pairs={{0,7},{1,4},{2,5},{3,6},{4,3},{5,0},{6,1},{7,2},{8,15},{9,12},{10,... | collective-permute-start | bytes 1572872 | tf_op jit(solution)/shard_map/ppermute | solution.py:191
  116.8 9.0 %collective-permute-done.18.refs_3_ = bf16[128,16,128]{2,1,0:T(8,128)(2,1)S(1)} collective-permute-done((bf16[128,16,128]{2,1,0:T(8,128)(2,1)}, bf16[128,16,128]{2,1,0:T(8,128)(2,1)S(1)}, u32[]{:S(2)}, u32[]{:S(2)}) %collective-permute-start.18) | collective-permute-done | bytes 524320 | tf_op jit(solution)/shard_map/ppermute | solution.py:191
  125.8 11.7 %collective-permute-done.19.refs_4_ = bf16[128,16,128]{2,1,0:T(8,128)(2,1)S(1)} collective-permute-done((bf16[128,16,128]{2,1,0:T(8,128)(2,1)}, bf16[128,16,128]{2,1,0:T(8,128)(2,1)S(1)}, u32[]{:S(2)}, u32[]{:S(2)}) %collective-permute-start.19) | collective-permute-done | bytes 524320 | tf_op jit(solution)/shard_map/ppermute | solution.py:191
  137.5 11.5 %collective-permute-done.20.refs_5_ = bf16[128,16,128]{2,1,0:T(8,128)(2,1)S(1)} collective-permute-done((bf16[128,16,128]{2,1,0:T(8,128)(2,1)}, bf16[128,16,128]{2,1,0:T(8,128)(2,1)S(1)}, u32[]{:S(2)}, u32[]{:S(2)}) %collective-permute-start.20) | collective-permute-done | bytes 524320 | tf_op jit(solution)/shard_map/ppermute | solution.py:191
  149.1 3.1 %collective-permute-done.22.refs_7_ = bf16[128,16,128]{2,1,0:T(8,128)(2,1)} collective-permute-done((bf16[128,16,128]{2,1,0:T(8,128)(2,1)}, bf16[128,16,128]{2,1,0:T(8,128)(2,1)}, u32[]{:S(2)}, u32[]{:S(2)}) %collective-permute-start.22) | collective-permute-done | bytes 524320 | tf_op jit(solution)/shard_map/ppermute | solution.py:191
  152.2 12.8 %sums_part.4 = f32[128,5,16,128]{3,2,1,0:T(8,128)} custom-call(s32[8,128]{1,0:T(8,128)} %stack.17.patch_ref, bf16[128,16,128]{2,1,0:T(8,128)(2,1)} %get-tuple-element.159.refs_0_, bf16[128,16,128]{2,1,0:T(8,128)(2,1)} %copy-done.8, bf16[128,16,128]{2,1,0:T(8,128)(2,1)} %copy-done.9, bf16[128,16,128]{2,1,0:T(8,128)(2,1)} %copy-done.10, ...), custom_call_target="tpu_custom_call" | custom-call | flops 104857600 | bytes 5242880 | tf_op jit(solution)/shard_map/sums_part/pallas_call | solution.py:126
  165.2 0.8 copy-done.34
  167.0 3.5 %collective-permute-start.26 = (bf16[128,8,128]{2,1,0:T(8,128)(2,1)S(1)}, bf16[128,8,128]{2,1,0:T(8,128)(2,1)S(1)}, u32[]{:S(2)}, u32[]{:S(2)}) collective-permute-start(bf16[128,8,128]{2,1,0:T(8,128)(2,1)S(1)} %copy-done.31), channel_id=1, source_target_pairs={{0,2},{1,3},{2,0},{3,1},{4,6},{5,7},{6,4},{7,5},{8,10},{9,11},{10,... | collective-permute-start | bytes 786440 | tf_op jit(solution)/shard_map/ppermute | solution.py:191
  170.6 2.6 collective-permute-start.28
  173.2 1.6 collective-permute-done.24.refs_2_
  174.7 3.2 %collective-permute-start.29 = (bf16[128,8,128]{2,1,0:T(8,128)(2,1)S(1)}, bf16[128,8,128]{2,1,0:T(8,128)(2,1)S(1)}, u32[]{:S(2)}, u32[]{:S(2)}) collective-permute-start(bf16[128,8,128]{2,1,0:T(8,128)(2,1)S(1)} %copy-done.28), channel_id=1, source_target_pairs={{0,7},{1,4},{2,5},{3,6},{4,3},{5,0},{6,1},{7,2},{8,15},{9,12},{10,... | collective-permute-start | bytes 786440 | tf_op jit(solution)/shard_map/ppermute | solution.py:191
  177.9 3.4 %collective-permute-done.25.refs_3_ = bf16[128,8,128]{2,1,0:T(8,128)(2,1)S(1)} collective-permute-done((bf16[128,8,128]{2,1,0:T(8,128)(2,1)S(1)}, bf16[128,8,128]{2,1,0:T(8,128)(2,1)S(1)}, u32[]{:S(2)}, u32[]{:S(2)}) %collective-permute-start.25) | collective-permute-done | bytes 262176 | tf_op jit(solution)/shard_map/ppermute | solution.py:191
  181.3 6.1 %collective-permute-done.26.refs_4_ = bf16[128,8,128]{2,1,0:T(8,128)(2,1)S(1)} collective-permute-done((bf16[128,8,128]{2,1,0:T(8,128)(2,1)S(1)}, bf16[128,8,128]{2,1,0:T(8,128)(2,1)S(1)}, u32[]{:S(2)}, u32[]{:S(2)}) %collective-permute-start.26) | collective-permute-done | bytes 262176 | tf_op jit(solution)/shard_map/ppermute | solution.py:191
  187.5 5.9 %collective-permute-done.27.refs_5_ = bf16[128,8,128]{2,1,0:T(8,128)(2,1)S(1)} collective-permute-done((bf16[128,8,128]{2,1,0:T(8,128)(2,1)S(1)}, bf16[128,8,128]{2,1,0:T(8,128)(2,1)S(1)}, u32[]{:S(2)}, u32[]{:S(2)}) %collective-permute-start.27) | collective-permute-done | bytes 262176 | tf_op jit(solution)/shard_map/ppermute | solution.py:191
  194.9 7.0 %sums_part.5 = f32[128,5,8,128]{3,2,1,0:T(8,128)S(1)} custom-call(s32[8,128]{1,0:T(8,128)} %stack.17.patch_ref, bf16[128,8,128]{2,1,0:T(8,128)(2,1)} %get-tuple-element.167.refs_0_, bf16[128,8,128]{2,1,0:T(8,128)(2,1)} %copy-done.16, bf16[128,8,128]{2,1,0:T(8,128)(2,1)} %copy-done.17, bf16[128,8,128]{2,1,0:T(8,128)(2,1)} %copy-done.18, ...), custom_call_target="tpu_custom_call" | custom-call | flops 52428800 | bytes 2621440 | tf_op jit(solution)/shard_map/sums_part/pallas_call | solution.py:126
  202.1 14.6 %collective-permute-done.30 = f32[8,5,8,128]{3,2,1,0:T(8,128)S(1)} collective-permute-done((f32[8,5,8,128]{3,2,1,0:T(8,128)S(1)}, f32[8,5,8,128]{3,2,1,0:T(8,128)S(1)}, u32[]{:S(2)}, u32[]{:S(2)}) %collective-permute-start.30) | collective-permute-done | bytes 163872 | tf_op jit(solution)/shard_map/ppermute | solution.py:148
  216.6 54.2 %while.16 = (s32[]{:T(128)}, f32[8,5,8,128]{3,2,1,0:T(8,128)S(1)}, f32[8,5,8,128]{3,2,1,0:T(8,128)S(1)}, s32[]{:T(128)}, f32[128,5,8,128]{3,2,1,0:T(8,128)S(1)},...) while((s32[]{:T(128)}, f32[8,5,8,128]{3,2,1,0:T(8,128)S(1)}, ...), condition=%wide.region_3.0_spmd, body=%wide.region_2.0_spmd.sunk | while | flops 81948 | bytes 2294243 | solution.py:156
  216.9 2.6 collective-permute-start.1
  219.5 8.1 %collective-permute-done = f32[8,5,8,128]{3,2,1,0:T(8,128)S(1)} collective-permute-done((f32[8,5,8,128]{3,2,1,0:T(8,128)S(1)}, f32[8,5,8,128]{3,2,1,0:T(8,128)S(1)}, u32[]{:S(2)}, u32[]{:S(2)}) %collective-permute-start) | collective-permute-done | bytes 163872 | tf_op jit(solution)/shard_map/while/body/eval_jaxpr/ppermute | solution.py:148
  227.8 2.6 collective-permute-start.1
  230.4 7.6 %collective-permute-done = f32[8,5,8,128]{3,2,1,0:T(8,128)S(1)} collective-permute-done((f32[8,5,8,128]{3,2,1,0:T(8,128)S(1)}, f32[8,5,8,128]{3,2,1,0:T(8,128)S(1)}, u32[]{:S(2)}, u32[]{:S(2)}) %collective-permute-start) | collective-permute-done | bytes 163872 | tf_op jit(solution)/shard_map/while/body/eval_jaxpr/ppermute | solution.py:148
  238.3 2.6 collective-permute-start.1
  240.9 6.7 %collective-permute-done = f32[8,5,8,128]{3,2,1,0:T(8,128)S(1)} collective-permute-done((f32[8,5,8,128]{3,2,1,0:T(8,128)S(1)}, f32[8,5,8,128]{3,2,1,0:T(8,128)S(1)}, u32[]{:S(2)}, u32[]{:S(2)}) %collective-permute-start) | collective-permute-done | bytes 163872 | tf_op jit(solution)/shard_map/while/body/eval_jaxpr/ppermute | solution.py:148
  247.8 2.6 collective-permute-start.1
  250.5 2.9 %collective-permute-done = f32[8,5,8,128]{3,2,1,0:T(8,128)S(1)} collective-permute-done((f32[8,5,8,128]{3,2,1,0:T(8,128)S(1)}, f32[8,5,8,128]{3,2,1,0:T(8,128)S(1)}, u32[]{:S(2)}, u32[]{:S(2)}) %collective-permute-start) | collective-permute-done | bytes 163872 | tf_op jit(solution)/shard_map/while/body/eval_jaxpr/ppermute | solution.py:148
  254.2 2.2 collective-permute-start.1
  256.4 2.7 collective-permute-done
  259.3 2.8 collective-permute-start.1
  262.1 2.6 collective-permute-done
  264.8 2.9 collective-permute-start.1
  267.7 3.1 %collective-permute-done = f32[8,5,8,128]{3,2,1,0:T(8,128)S(1)} collective-permute-done((f32[8,5,8,128]{3,2,1,0:T(8,128)S(1)}, f32[8,5,8,128]{3,2,1,0:T(8,128)S(1)}, u32[]{:S(2)}, u32[]{:S(2)}) %collective-permute-start) | collective-permute-done | bytes 163872 | tf_op jit(solution)/shard_map/while/body/eval_jaxpr/ppermute | solution.py:148
  271.0 0.8 divide_add_fusion.2
  271.8 0.9 fusion.13
  272.7 1.0 divide_add_fusion
  273.6 1.0 fusion.4
  274.8 6.7 %collective-permute-start.31 = (f32[4,4,16,256]{3,2,1,0:T(8,128)S(1)}, f32[4,4,16,256]{3,2,1,0:T(8,128)S(1)}, u32[]{:S(2)}, u32[]{:S(2)}) collective-permute-start(f32[4,4,16,256]{3,2,1,0:T(8,128)S(1)} %dynamic-slice_bitcast_fusion), channel_id=1, source_target_pairs={{0,4},{4,0},{1,5},{5,1},{2,6},{6,2},{3,7},{7,3},{8,12},{12,8},{9,1... | collective-permute-start | bytes 786440 | tf_op jit(solution)/shard_map/ppermute | solution.py:235
  281.5 1.2 collective-permute-done.31
  282.7 0.9 pad_maximum_fusion
  (146 shorter events, 9.2 us)
Async XLA Ops:
  7.2 263.8 %reduce-scatter.3.cloned.1.call-start = ((), (), s32[]{:S(2)}) async-start(), calls=%async_computation.2 | async-start | bytes 2785280 | tf_op jit(solution)/shard_map/reduce_scatter | solution.py:217
  11.9 49.6 %copy-start = (s32[136,256]{1,0:T(8,128)}, s32[136,256]{1,0:T(8,128)S(1)}, u32[]{:S(2)}) copy-start(s32[136,256]{1,0:T(8,128)S(1)} %get-tuple-element.142.refs_8_) | copy-start | bytes 417796
  11.9 31.9 %collective-permute-start.2 = (s32[136,256]{1,0:T(8,128)S(1)}, s32[136,256]{1,0:T(8,128)S(1)}, u32[]{:S(2)}, u32[]{:S(2)}) collective-permute-start(s32[136,256]{1,0:T(8,128)S(1)} %get-tuple-element.143), channel_id=1, source_target_pairs={{0,4},{1,5},{2,6},{3,7},{4,0},{5,1},{6,2},{7,3},{8,12},{9,13},{10,... | collective-permute-start | bytes 417800 | tf_op jit(solution)/shard_map/ppermute | solution.py:191
  32.5 11.4 %collective-permute-start.3 = (s32[136,256]{1,0:T(8,128)S(1)}, s32[136,256]{1,0:T(8,128)S(1)}, u32[]{:S(2)}, u32[]{:S(2)}) collective-permute-start(s32[136,256]{1,0:T(8,128)S(1)} %get-tuple-element.144), channel_id=1, source_target_pairs={{0,1},{1,2},{2,3},{3,0},{4,5},{5,6},{6,7},{7,4},{8,9},{9,10},{10,1... | collective-permute-start | bytes 417800 | tf_op jit(solution)/shard_map/ppermute | solution.py:191
  32.5 12.6 %collective-permute-start.4 = (s32[136,256]{1,0:T(8,128)S(1)}, s32[136,256]{1,0:T(8,128)S(1)}, u32[]{:S(2)}, u32[]{:S(2)}) collective-permute-start(s32[136,256]{1,0:T(8,128)S(1)} %get-tuple-element.145), channel_id=1, source_target_pairs={{0,5},{1,6},{2,7},{3,4},{4,1},{5,2},{6,3},{7,0},{8,13},{9,14},{10,... | collective-permute-start | bytes 417800 | tf_op jit(solution)/shard_map/ppermute | solution.py:191
  32.5 14.2 %collective-permute-start.5 = (s32[136,256]{1,0:T(8,128)S(1)}, s32[136,256]{1,0:T(8,128)S(1)}, u32[]{:S(2)}, u32[]{:S(2)}) collective-permute-start(s32[136,256]{1,0:T(8,128)S(1)} %get-tuple-element.146), channel_id=1, source_target_pairs={{0,2},{1,3},{2,0},{3,1},{4,6},{5,7},{6,4},{7,5},{8,10},{9,11},{10,... | collective-permute-start | bytes 417800 | tf_op jit(solution)/shard_map/ppermute | solution.py:191
  43.3 15.1 %collective-permute-start.9 = (bf16[128,8,128]{2,1,0:T(8,128)(2,1)}, bf16[128,8,128]{2,1,0:T(8,128)(2,1)S(1)}, u32[]{:S(2)}, u32[]{:S(2)}) collective-permute-start(bf16[128,8,128]{2,1,0:T(8,128)(2,1)} %get-tuple-element.152), channel_id=1, source_target_pairs={{0,4},{1,5},{2,6},{3,7},{4,0},{5,1},{6,2},{7,3},{8,12},{9,13},{10,... | collective-permute-start | bytes 786440 | tf_op jit(solution)/shard_map/ppermute | solution.py:191
  43.8 36.5 %copy-start.1 = (s32[136,256]{1,0:T(8,128)}, s32[136,256]{1,0:T(8,128)S(1)}, u32[]{:S(2)}) copy-start(s32[136,256]{1,0:T(8,128)S(1)} %collective-permute-done.2.refs_9_) | copy-start | bytes 417796
  43.8 16.8 %collective-permute-start.10 = (bf16[128,8,128]{2,1,0:T(8,128)(2,1)}, bf16[128,8,128]{2,1,0:T(8,128)(2,1)S(1)}, u32[]{:S(2)}, u32[]{:S(2)}) collective-permute-start(bf16[128,8,128]{2,1,0:T(8,128)(2,1)} %get-tuple-element.153), channel_id=1, source_target_pairs={{0,1},{1,2},{2,3},{3,0},{4,5},{5,6},{6,7},{7,4},{8,9},{9,10},{10,1... | collective-permute-start | bytes 786440 | tf_op jit(solution)/shard_map/ppermute | solution.py:191
  43.9 36.5 %copy-start.2 = (s32[136,256]{1,0:T(8,128)}, s32[136,256]{1,0:T(8,128)S(1)}, u32[]{:S(2)}) copy-start(s32[136,256]{1,0:T(8,128)S(1)} %collective-permute-done.3.refs_10_) | copy-start | bytes 417796
  43.9 9.6 %collective-permute-start.6 = (s32[136,256]{1,0:T(8,128)S(1)}, s32[136,256]{1,0:T(8,128)S(1)}, u32[]{:S(2)}, u32[]{:S(2)}) collective-permute-start(s32[136,256]{1,0:T(8,128)S(1)} %get-tuple-element.147), channel_id=1, source_target_pairs={{0,6},{1,7},{2,4},{3,5},{4,2},{5,3},{6,0},{7,1},{8,14},{9,15},{10,... | collective-permute-start | bytes 417800 | tf_op jit(solution)/shard_map/ppermute | solution.py:191
  45.1 35.3 %copy-start.3 = (s32[136,256]{1,0:T(8,128)}, s32[136,256]{1,0:T(8,128)S(1)}, u32[]{:S(2)}) copy-start(s32[136,256]{1,0:T(8,128)S(1)} %collective-permute-done.4.refs_11_) | copy-start | bytes 417796
  45.1 9.4 %collective-permute-start.7 = (s32[136,256]{1,0:T(8,128)S(1)}, s32[136,256]{1,0:T(8,128)S(1)}, u32[]{:S(2)}, u32[]{:S(2)}) collective-permute-start(s32[136,256]{1,0:T(8,128)S(1)} %get-tuple-element.148), channel_id=1, source_target_pairs={{0,3},{1,0},{2,1},{3,2},{4,7},{5,4},{6,5},{7,6},{8,11},{9,8},{10,9... | collective-permute-start | bytes 417800 | tf_op jit(solution)/shard_map/ppermute | solution.py:191
  46.7 33.7 %copy-start.4 = (s32[136,256]{1,0:T(8,128)}, s32[136,256]{1,0:T(8,128)S(1)}, u32[]{:S(2)}) copy-start(s32[136,256]{1,0:T(8,128)S(1)} %collective-permute-done.5.refs_12_) | copy-start | bytes 417796
  46.7 11.0 %collective-permute-start.8 = (s32[136,256]{1,0:T(8,128)S(1)}, s32[136,256]{1,0:T(8,128)S(1)}, u32[]{:S(2)}, u32[]{:S(2)}) collective-permute-start(s32[136,256]{1,0:T(8,128)S(1)} %get-tuple-element.149), channel_id=1, source_target_pairs={{0,7},{1,4},{2,5},{3,6},{4,3},{5,0},{6,1},{7,2},{8,15},{9,12},{10,... | collective-permute-start | bytes 417800 | tf_op jit(solution)/shard_map/ppermute | solution.py:191
  53.5 26.9 %copy-start.5 = (s32[136,256]{1,0:T(8,128)}, s32[136,256]{1,0:T(8,128)S(1)}, u32[]{:S(2)}) copy-start(s32[136,256]{1,0:T(8,128)S(1)} %collective-permute-done.6.refs_13_) | copy-start | bytes 417796
  53.5 9.4 %collective-permute-start.11 = (bf16[128,8,128]{2,1,0:T(8,128)(2,1)}, bf16[128,8,128]{2,1,0:T(8,128)(2,1)S(1)}, u32[]{:S(2)}, u32[]{:S(2)}) collective-permute-start(bf16[128,8,128]{2,1,0:T(8,128)(2,1)} %get-tuple-element.154), channel_id=1, source_target_pairs={{0,5},{1,6},{2,7},{3,4},{4,1},{5,2},{6,3},{7,0},{8,13},{9,14},{10,... | collective-permute-start | bytes 786440 | tf_op jit(solution)/shard_map/ppermute | solution.py:191
  54.4 26.0 %copy-start.6 = (s32[136,256]{1,0:T(8,128)}, s32[136,256]{1,0:T(8,128)S(1)}, u32[]{:S(2)}) copy-start(s32[136,256]{1,0:T(8,128)S(1)} %collective-permute-done.7.refs_14_) | copy-start | bytes 417796
  54.4 14.3 %collective-permute-start.12 = (bf16[128,8,128]{2,1,0:T(8,128)(2,1)}, bf16[128,8,128]{2,1,0:T(8,128)(2,1)S(1)}, u32[]{:S(2)}, u32[]{:S(2)}) collective-permute-start(bf16[128,8,128]{2,1,0:T(8,128)(2,1)} %get-tuple-element.155), channel_id=1, source_target_pairs={{0,2},{1,3},{2,0},{3,1},{4,6},{5,7},{6,4},{7,5},{8,10},{9,11},{10,... | collective-permute-start | bytes 786440 | tf_op jit(solution)/shard_map/ppermute | solution.py:191
  57.7 22.8 %copy-start.7 = (s32[136,256]{1,0:T(8,128)}, s32[136,256]{1,0:T(8,128)S(1)}, u32[]{:S(2)}) copy-start(s32[136,256]{1,0:T(8,128)S(1)} %collective-permute-done.8.refs_15_) | copy-start | bytes 417796
  57.7 16.9 %collective-permute-start.13 = (bf16[128,8,128]{2,1,0:T(8,128)(2,1)}, bf16[128,8,128]{2,1,0:T(8,128)(2,1)S(1)}, u32[]{:S(2)}, u32[]{:S(2)}) collective-permute-start(bf16[128,8,128]{2,1,0:T(8,128)(2,1)} %get-tuple-element.156), channel_id=1, source_target_pairs={{0,6},{1,7},{2,4},{3,5},{4,2},{5,3},{6,0},{7,1},{8,14},{9,15},{10,... | collective-permute-start | bytes 786440 | tf_op jit(solution)/shard_map/ppermute | solution.py:191
  58.5 22.0 %copy-start.14 = (bf16[128,8,128]{2,1,0:T(8,128)(2,1)}, bf16[128,8,128]{2,1,0:T(8,128)(2,1)S(1)}, u32[]{:S(2)}) copy-start(bf16[128,8,128]{2,1,0:T(8,128)(2,1)S(1)} %collective-permute-done.9.refs_1_) | copy-start | bytes 786436
  58.5 16.1 %collective-permute-start.14 = (bf16[128,8,128]{2,1,0:T(8,128)(2,1)}, bf16[128,8,128]{2,1,0:T(8,128)(2,1)S(1)}, u32[]{:S(2)}, u32[]{:S(2)}) collective-permute-start(bf16[128,8,128]{2,1,0:T(8,128)(2,1)} %get-tuple-element.157), channel_id=1, source_target_pairs={{0,3},{1,0},{2,1},{3,2},{4,7},{5,4},{6,5},{7,6},{8,11},{9,8},{10,9... | collective-permute-start | bytes 786440 | tf_op jit(solution)/shard_map/ppermute | solution.py:191
  60.7 19.8 %copy-start.15 = (bf16[128,8,128]{2,1,0:T(8,128)(2,1)}, bf16[128,8,128]{2,1,0:T(8,128)(2,1)S(1)}, u32[]{:S(2)}) copy-start(bf16[128,8,128]{2,1,0:T(8,128)(2,1)S(1)} %collective-permute-done.10.refs_2_) | copy-start | bytes 786436
  60.7 19.7 %collective-permute-start.15 = (bf16[128,8,128]{2,1,0:T(8,128)(2,1)}, bf16[128,8,128]{2,1,0:T(8,128)(2,1)S(1)}, u32[]{:S(2)}, u32[]{:S(2)}) collective-permute-start(bf16[128,8,128]{2,1,0:T(8,128)(2,1)} %get-tuple-element.158), channel_id=1, source_target_pairs={{0,7},{1,4},{2,5},{3,6},{4,3},{5,0},{6,1},{7,2},{8,15},{9,12},{10,... | collective-permute-start | bytes 786440 | tf_op jit(solution)/shard_map/ppermute | solution.py:191
  63.0 17.5 %copy-start.22 = (bf16[128,8,128]{2,1,0:T(8,128)(2,1)}, bf16[128,8,128]{2,1,0:T(8,128)(2,1)S(1)}, u32[]{:S(2)}) copy-start(bf16[128,8,128]{2,1,0:T(8,128)(2,1)S(1)} %collective-permute-done.11.refs_3_) | copy-start | bytes 786436
  89.6 183.0 %reduce-scatter.5.cloned.1.call-start = ((), (), s32[]{:S(2)}) async-start(), calls=%async_computation.3 | async-start | bytes 5570560 | tf_op jit(solution)/shard_map/reduce_scatter | solution.py:217
  98.6 7.0 %collective-permute-start.16 = (bf16[128,16,128]{2,1,0:T(8,128)(2,1)}, bf16[128,16,128]{2,1,0:T(8,128)(2,1)S(1)}, u32[]{:S(2)}, u32[]{:S(2)}) collective-permute-start(bf16[128,16,128]{2,1,0:T(8,128)(2,1)} %get-tuple-element.160), channel_id=1, source_target_pairs={{0,4},{1,5},{2,6},{3,7},{4,0},{5,1},{6,2},{7,3},{8,12},{9,13},{10,... | collective-permute-start | bytes 1572872 | tf_op jit(solution)/shard_map/ppermute | solution.py:191
  98.8 15.1 %collective-permute-start.17 = (bf16[128,16,128]{2,1,0:T(8,128)(2,1)}, bf16[128,16,128]{2,1,0:T(8,128)(2,1)S(1)}, u32[]{:S(2)}, u32[]{:S(2)}) collective-permute-start(bf16[128,16,128]{2,1,0:T(8,128)(2,1)} %get-tuple-element.161), channel_id=1, source_target_pairs={{0,1},{1,2},{2,3},{3,0},{4,5},{5,6},{6,7},{7,4},{8,9},{9,10},{10,1... | collective-permute-start | bytes 1572872 | tf_op jit(solution)/shard_map/ppermute | solution.py:191
  102.1 23.8 %collective-permute-start.18 = (bf16[128,16,128]{2,1,0:T(8,128)(2,1)}, bf16[128,16,128]{2,1,0:T(8,128)(2,1)S(1)}, u32[]{:S(2)}, u32[]{:S(2)}) collective-permute-start(bf16[128,16,128]{2,1,0:T(8,128)(2,1)} %get-tuple-element.162), channel_id=1, source_target_pairs={{0,5},{1,6},{2,7},{3,4},{4,1},{5,2},{6,3},{7,0},{8,13},{9,14},{10,... | collective-permute-start | bytes 1572872 | tf_op jit(solution)/shard_map/ppermute | solution.py:191
  102.5 35.1 %collective-permute-start.19 = (bf16[128,16,128]{2,1,0:T(8,128)(2,1)}, bf16[128,16,128]{2,1,0:T(8,128)(2,1)S(1)}, u32[]{:S(2)}, u32[]{:S(2)}) collective-permute-start(bf16[128,16,128]{2,1,0:T(8,128)(2,1)} %get-tuple-element.163), channel_id=1, source_target_pairs={{0,2},{1,3},{2,0},{3,1},{4,6},{5,7},{6,4},{7,5},{8,10},{9,11},{10,... | collective-permute-start | bytes 1572872 | tf_op jit(solution)/shard_map/ppermute | solution.py:191
  103.3 45.8 %collective-permute-start.20 = (bf16[128,16,128]{2,1,0:T(8,128)(2,1)}, bf16[128,16,128]{2,1,0:T(8,128)(2,1)S(1)}, u32[]{:S(2)}, u32[]{:S(2)}) collective-permute-start(bf16[128,16,128]{2,1,0:T(8,128)(2,1)} %get-tuple-element.164), channel_id=1, source_target_pairs={{0,6},{1,7},{2,4},{3,5},{4,2},{5,3},{6,0},{7,1},{8,14},{9,15},{10,... | collective-permute-start | bytes 1572872 | tf_op jit(solution)/shard_map/ppermute | solution.py:191
  105.6 46.5 %copy-start.8 = (bf16[128,16,128]{2,1,0:T(8,128)(2,1)}, bf16[128,16,128]{2,1,0:T(8,128)(2,1)S(1)}, u32[]{:S(2)}) copy-start(bf16[128,16,128]{2,1,0:T(8,128)(2,1)S(1)} %collective-permute-done.16.refs_1_) | copy-start | bytes 1572868
  105.6 43.4 %collective-permute-start.21 = (bf16[128,16,128]{2,1,0:T(8,128)(2,1)}, bf16[128,16,128]{2,1,0:T(8,128)(2,1)S(1)}, u32[]{:S(2)}, u32[]{:S(2)}) collective-permute-start(bf16[128,16,128]{2,1,0:T(8,128)(2,1)} %get-tuple-element.165), channel_id=1, source_target_pairs={{0,3},{1,0},{2,1},{3,2},{4,7},{5,4},{6,5},{7,6},{8,11},{9,8},{10,9... | collective-permute-start | bytes 1572872 | tf_op jit(solution)/shard_map/ppermute | solution.py:191
  113.9 38.3 %copy-start.9 = (bf16[128,16,128]{2,1,0:T(8,128)(2,1)}, bf16[128,16,128]{2,1,0:T(8,128)(2,1)S(1)}, u32[]{:S(2)}) copy-start(bf16[128,16,128]{2,1,0:T(8,128)(2,1)S(1)} %collective-permute-done.17.refs_2_) | copy-start | bytes 1572868
  113.9 38.3 %collective-permute-start.22 = (bf16[128,16,128]{2,1,0:T(8,128)(2,1)}, bf16[128,16,128]{2,1,0:T(8,128)(2,1)}, u32[]{:S(2)}, u32[]{:S(2)}) collective-permute-start(bf16[128,16,128]{2,1,0:T(8,128)(2,1)} %get-tuple-element.166), channel_id=1, source_target_pairs={{0,7},{1,4},{2,5},{3,6},{4,3},{5,0},{6,1},{7,2},{8,15},{9,12},{10,... | collective-permute-start | bytes 1572872 | tf_op jit(solution)/shard_map/ppermute | solution.py:191
  125.8 26.4 %copy-start.10 = (bf16[128,16,128]{2,1,0:T(8,128)(2,1)}, bf16[128,16,128]{2,1,0:T(8,128)(2,1)S(1)}, u32[]{:S(2)}) copy-start(bf16[128,16,128]{2,1,0:T(8,128)(2,1)S(1)} %collective-permute-done.18.refs_3_) | copy-start | bytes 1572868
  137.5 14.7 %copy-start.11 = (bf16[128,16,128]{2,1,0:T(8,128)(2,1)}, bf16[128,16,128]{2,1,0:T(8,128)(2,1)S(1)}, u32[]{:S(2)}) copy-start(bf16[128,16,128]{2,1,0:T(8,128)(2,1)S(1)} %collective-permute-done.19.refs_4_) | copy-start | bytes 1572868
  166.0 4.6 %collective-permute-start.23 = (bf16[128,8,128]{2,1,0:T(8,128)(2,1)S(1)}, bf16[128,8,128]{2,1,0:T(8,128)(2,1)S(1)}, u32[]{:S(2)}, u32[]{:S(2)}) collective-permute-start(bf16[128,8,128]{2,1,0:T(8,128)(2,1)S(1)} %copy-done.34), channel_id=1, source_target_pairs={{0,4},{1,5},{2,6},{3,7},{4,0},{5,1},{6,2},{7,3},{8,12},{9,13},{10,... | collective-permute-start | bytes 786440 | tf_op jit(solution)/shard_map/ppermute | solution.py:191
  166.1 8.7 %collective-permute-start.24 = (bf16[128,8,128]{2,1,0:T(8,128)(2,1)S(1)}, bf16[128,8,128]{2,1,0:T(8,128)(2,1)S(1)}, u32[]{:S(2)}, u32[]{:S(2)}) collective-permute-start(bf16[128,8,128]{2,1,0:T(8,128)(2,1)S(1)} %copy-done.33), channel_id=1, source_target_pairs={{0,1},{1,2},{2,3},{3,0},{4,5},{5,6},{6,7},{7,4},{8,9},{9,10},{10,1... | collective-permute-start | bytes 786440 | tf_op jit(solution)/shard_map/ppermute | solution.py:191
  166.6 14.7 %collective-permute-start.25 = (bf16[128,8,128]{2,1,0:T(8,128)(2,1)S(1)}, bf16[128,8,128]{2,1,0:T(8,128)(2,1)S(1)}, u32[]{:S(2)}, u32[]{:S(2)}) collective-permute-start(bf16[128,8,128]{2,1,0:T(8,128)(2,1)S(1)} %copy-done.32), channel_id=1, source_target_pairs={{0,5},{1,6},{2,7},{3,4},{4,1},{5,2},{6,3},{7,0},{8,13},{9,14},{10,... | collective-permute-start | bytes 786440 | tf_op jit(solution)/shard_map/ppermute | solution.py:191
  167.0 20.5 %collective-permute-start.26 = (bf16[128,8,128]{2,1,0:T(8,128)(2,1)S(1)}, bf16[128,8,128]{2,1,0:T(8,128)(2,1)S(1)}, u32[]{:S(2)}, u32[]{:S(2)}) collective-permute-start(bf16[128,8,128]{2,1,0:T(8,128)(2,1)S(1)} %copy-done.31), channel_id=1, source_target_pairs={{0,2},{1,3},{2,0},{3,1},{4,6},{5,7},{6,4},{7,5},{8,10},{9,11},{10,... | collective-permute-start | bytes 786440 | tf_op jit(solution)/shard_map/ppermute | solution.py:191
  170.5 22.8 %collective-permute-start.27 = (bf16[128,8,128]{2,1,0:T(8,128)(2,1)S(1)}, bf16[128,8,128]{2,1,0:T(8,128)(2,1)S(1)}, u32[]{:S(2)}, u32[]{:S(2)}) collective-permute-start(bf16[128,8,128]{2,1,0:T(8,128)(2,1)S(1)} %copy-done.30), channel_id=1, source_target_pairs={{0,6},{1,7},{2,4},{3,5},{4,2},{5,3},{6,0},{7,1},{8,14},{9,15},{10,... | collective-permute-start | bytes 786440 | tf_op jit(solution)/shard_map/ppermute | solution.py:191
  170.5 24.3 %copy-start.16 = (bf16[128,8,128]{2,1,0:T(8,128)(2,1)}, bf16[128,8,128]{2,1,0:T(8,128)(2,1)S(1)}, u32[]{:S(2)}) copy-start(bf16[128,8,128]{2,1,0:T(8,128)(2,1)S(1)} %collective-permute-done.23.refs_1_) | copy-start | bytes 786436
  170.6 22.8 %collective-permute-start.28 = (bf16[128,8,128]{2,1,0:T(8,128)(2,1)S(1)}, bf16[128,8,128]{2,1,0:T(8,128)(2,1)S(1)}, u32[]{:S(2)}, u32[]{:S(2)}) collective-permute-start(bf16[128,8,128]{2,1,0:T(8,128)(2,1)S(1)} %copy-done.29), channel_id=1, source_target_pairs={{0,3},{1,0},{2,1},{3,2},{4,7},{5,4},{6,5},{7,6},{8,11},{9,8},{10,9... | collective-permute-start | bytes 786440 | tf_op jit(solution)/shard_map/ppermute | solution.py:191
  174.7 20.2 %copy-start.17 = (bf16[128,8,128]{2,1,0:T(8,128)(2,1)}, bf16[128,8,128]{2,1,0:T(8,128)(2,1)S(1)}, u32[]{:S(2)}) copy-start(bf16[128,8,128]{2,1,0:T(8,128)(2,1)S(1)} %collective-permute-done.24.refs_2_) | copy-start | bytes 786436
  174.7 19.3 %collective-permute-start.29 = (bf16[128,8,128]{2,1,0:T(8,128)(2,1)S(1)}, bf16[128,8,128]{2,1,0:T(8,128)(2,1)S(1)}, u32[]{:S(2)}, u32[]{:S(2)}) collective-permute-start(bf16[128,8,128]{2,1,0:T(8,128)(2,1)S(1)} %copy-done.28), channel_id=1, source_target_pairs={{0,7},{1,4},{2,5},{3,6},{4,3},{5,0},{6,1},{7,2},{8,15},{9,12},{10,... | collective-permute-start | bytes 786440 | tf_op jit(solution)/shard_map/ppermute | solution.py:191
  181.3 13.6 %copy-start.18 = (bf16[128,8,128]{2,1,0:T(8,128)(2,1)}, bf16[128,8,128]{2,1,0:T(8,128)(2,1)S(1)}, u32[]{:S(2)}) copy-start(bf16[128,8,128]{2,1,0:T(8,128)(2,1)S(1)} %collective-permute-done.25.refs_3_) | copy-start | bytes 786436
  201.9 14.7 %collective-permute-start.30 = (f32[8,5,8,128]{3,2,1,0:T(8,128)S(1)}, f32[8,5,8,128]{3,2,1,0:T(8,128)S(1)}, u32[]{:S(2)}, u32[]{:S(2)}) collective-permute-start(f32[8,5,8,128]{3,2,1,0:T(8,128)S(1)} %constant_dynamic-slice_fusion), channel_id=1, source_target_pairs={{0,8},{8,16},{16,24},{24,32},{32,40},{40,48},{48,56},{56,64},{64,7... | collective-permute-start | bytes 491528 | tf_op jit(solution)/shard_map/ppermute | solution.py:148
  216.7 10.9 %collective-permute-start = (f32[8,5,8,128]{3,2,1,0:T(8,128)S(1)}, f32[8,5,8,128]{3,2,1,0:T(8,128)S(1)}, u32[]{:S(2)}, u32[]{:S(2)}) collective-permute-start(f32[8,5,8,128]{3,2,1,0:T(8,128)S(1)} %get-tuple-element.264), channel_id=1, source_target_pairs={{0,8},{8,16},{16,24},{24,32},{32,40},{40,48},{48,56},{56,64},{64,7... | collective-permute-start | bytes 491528 | tf_op jit(solution)/shard_map/while/body/eval_jaxpr/ppermute | solution.py:148
  216.9 10.7 %collective-permute-start.1 = (f32[8,5,8,128]{3,2,1,0:T(8,128)S(1)}, f32[8,5,8,128]{3,2,1,0:T(8,128)S(1)}, u32[]{:S(2)}, u32[]{:S(2)}) collective-permute-start(f32[8,5,8,128]{3,2,1,0:T(8,128)S(1)} %get-tuple-element.265), channel_id=1, source_target_pairs={{0,120},{8,0},{16,8},{24,16},{32,24},{40,32},{48,40},{56,48},{64,5... | collective-permute-start | bytes 491528 | tf_op jit(solution)/shard_map/while/body/eval_jaxpr/ppermute | solution.py:148
  227.6 10.4 %collective-permute-start = (f32[8,5,8,128]{3,2,1,0:T(8,128)S(1)}, f32[8,5,8,128]{3,2,1,0:T(8,128)S(1)}, u32[]{:S(2)}, u32[]{:S(2)}) collective-permute-start(f32[8,5,8,128]{3,2,1,0:T(8,128)S(1)} %get-tuple-element.264), channel_id=1, source_target_pairs={{0,8},{8,16},{16,24},{24,32},{32,40},{40,48},{48,56},{56,64},{64,7... | collective-permute-start | bytes 491528 | tf_op jit(solution)/shard_map/while/body/eval_jaxpr/ppermute | solution.py:148
  227.8 10.3 %collective-permute-start.1 = (f32[8,5,8,128]{3,2,1,0:T(8,128)S(1)}, f32[8,5,8,128]{3,2,1,0:T(8,128)S(1)}, u32[]{:S(2)}, u32[]{:S(2)}) collective-permute-start(f32[8,5,8,128]{3,2,1,0:T(8,128)S(1)} %get-tuple-element.265), channel_id=1, source_target_pairs={{0,120},{8,0},{16,8},{24,16},{32,24},{40,32},{48,40},{56,48},{64,5... | collective-permute-start | bytes 491528 | tf_op jit(solution)/shard_map/while/body/eval_jaxpr/ppermute | solution.py:148
  238.1 9.5 %collective-permute-start = (f32[8,5,8,128]{3,2,1,0:T(8,128)S(1)}, f32[8,5,8,128]{3,2,1,0:T(8,128)S(1)}, u32[]{:S(2)}, u32[]{:S(2)}) collective-permute-start(f32[8,5,8,128]{3,2,1,0:T(8,128)S(1)} %get-tuple-element.264), channel_id=1, source_target_pairs={{0,8},{8,16},{16,24},{24,32},{32,40},{40,48},{48,56},{56,64},{64,7... | collective-permute-start | bytes 491528 | tf_op jit(solution)/shard_map/while/body/eval_jaxpr/ppermute | solution.py:148
  238.3 9.4 %collective-permute-start.1 = (f32[8,5,8,128]{3,2,1,0:T(8,128)S(1)}, f32[8,5,8,128]{3,2,1,0:T(8,128)S(1)}, u32[]{:S(2)}, u32[]{:S(2)}) collective-permute-start(f32[8,5,8,128]{3,2,1,0:T(8,128)S(1)} %get-tuple-element.265), channel_id=1, source_target_pairs={{0,120},{8,0},{16,8},{24,16},{32,24},{40,32},{48,40},{56,48},{64,5... | collective-permute-start | bytes 491528 | tf_op jit(solution)/shard_map/while/body/eval_jaxpr/ppermute | solution.py:148
  247.7 5.7 %collective-permute-start = (f32[8,5,8,128]{3,2,1,0:T(8,128)S(1)}, f32[8,5,8,128]{3,2,1,0:T(8,128)S(1)}, u32[]{:S(2)}, u32[]{:S(2)}) collective-permute-start(f32[8,5,8,128]{3,2,1,0:T(8,128)S(1)} %get-tuple-element.264), channel_id=1, source_target_pairs={{0,8},{8,16},{16,24},{24,32},{32,40},{40,48},{48,56},{56,64},{64,7... | collective-permute-start | bytes 491528 | tf_op jit(solution)/shard_map/while/body/eval_jaxpr/ppermute | solution.py:148
  247.8 5.7 %collective-permute-start.1 = (f32[8,5,8,128]{3,2,1,0:T(8,128)S(1)}, f32[8,5,8,128]{3,2,1,0:T(8,128)S(1)}, u32[]{:S(2)}, u32[]{:S(2)}) collective-permute-start(f32[8,5,8,128]{3,2,1,0:T(8,128)S(1)} %get-tuple-element.265), channel_id=1, source_target_pairs={{0,120},{8,0},{16,8},{24,16},{32,24},{40,32},{48,40},{56,48},{64,5... | collective-permute-start | bytes 491528 | tf_op jit(solution)/shard_map/while/body/eval_jaxpr/ppermute | solution.py:148
  253.6 5.5 %collective-permute-start = (f32[8,5,8,128]{3,2,1,0:T(8,128)S(1)}, f32[8,5,8,128]{3,2,1,0:T(8,128)S(1)}, u32[]{:S(2)}, u32[]{:S(2)}) collective-permute-start(f32[8,5,8,128]{3,2,1,0:T(8,128)S(1)} %get-tuple-element.264), channel_id=1, source_target_pairs={{0,8},{8,16},{16,24},{24,32},{32,40},{40,48},{48,56},{56,64},{64,7... | collective-permute-start | bytes 491528 | tf_op jit(solution)/shard_map/while/body/eval_jaxpr/ppermute | solution.py:148
  254.2 4.9 %collective-permute-start.1 = (f32[8,5,8,128]{3,2,1,0:T(8,128)S(1)}, f32[8,5,8,128]{3,2,1,0:T(8,128)S(1)}, u32[]{:S(2)}, u32[]{:S(2)}) collective-permute-start(f32[8,5,8,128]{3,2,1,0:T(8,128)S(1)} %get-tuple-element.265), channel_id=1, source_target_pairs={{0,120},{8,0},{16,8},{24,16},{32,24},{40,32},{48,40},{56,48},{64,5... | collective-permute-start | bytes 491528 | tf_op jit(solution)/shard_map/while/body/eval_jaxpr/ppermute | solution.py:148
  259.1 5.5 %collective-permute-start = (f32[8,5,8,128]{3,2,1,0:T(8,128)S(1)}, f32[8,5,8,128]{3,2,1,0:T(8,128)S(1)}, u32[]{:S(2)}, u32[]{:S(2)}) collective-permute-start(f32[8,5,8,128]{3,2,1,0:T(8,128)S(1)} %get-tuple-element.264), channel_id=1, source_target_pairs={{0,8},{8,16},{16,24},{24,32},{32,40},{40,48},{48,56},{56,64},{64,7... | collective-permute-start | bytes 491528 | tf_op jit(solution)/shard_map/while/body/eval_jaxpr/ppermute | solution.py:148
  259.3 5.4 %collective-permute-start.1 = (f32[8,5,8,128]{3,2,1,0:T(8,128)S(1)}, f32[8,5,8,128]{3,2,1,0:T(8,128)S(1)}, u32[]{:S(2)}, u32[]{:S(2)}) collective-permute-start(f32[8,5,8,128]{3,2,1,0:T(8,128)S(1)} %get-tuple-element.265), channel_id=1, source_target_pairs={{0,120},{8,0},{16,8},{24,16},{32,24},{40,32},{48,40},{56,48},{64,5... | collective-permute-start | bytes 491528 | tf_op jit(solution)/shard_map/while/body/eval_jaxpr/ppermute | solution.py:148
  264.7 6.1 %collective-permute-start = (f32[8,5,8,128]{3,2,1,0:T(8,128)S(1)}, f32[8,5,8,128]{3,2,1,0:T(8,128)S(1)}, u32[]{:S(2)}, u32[]{:S(2)}) collective-permute-start(f32[8,5,8,128]{3,2,1,0:T(8,128)S(1)} %get-tuple-element.264), channel_id=1, source_target_pairs={{0,8},{8,16},{16,24},{24,32},{32,40},{40,48},{48,56},{56,64},{64,7... | collective-permute-start | bytes 491528 | tf_op jit(solution)/shard_map/while/body/eval_jaxpr/ppermute | solution.py:148
  264.8 6.0 %collective-permute-start.1 = (f32[8,5,8,128]{3,2,1,0:T(8,128)S(1)}, f32[8,5,8,128]{3,2,1,0:T(8,128)S(1)}, u32[]{:S(2)}, u32[]{:S(2)}) collective-permute-start(f32[8,5,8,128]{3,2,1,0:T(8,128)S(1)} %get-tuple-element.265), channel_id=1, source_target_pairs={{0,120},{8,0},{16,8},{24,16},{32,24},{40,32},{48,40},{56,48},{64,5... | collective-permute-start | bytes 491528 | tf_op jit(solution)/shard_map/while/body/eval_jaxpr/ppermute | solution.py:148
  274.8 7.8 %collective-permute-start.31 = (f32[4,4,16,256]{3,2,1,0:T(8,128)S(1)}, f32[4,4,16,256]{3,2,1,0:T(8,128)S(1)}, u32[]{:S(2)}, u32[]{:S(2)}) collective-permute-start(f32[4,4,16,256]{3,2,1,0:T(8,128)S(1)} %dynamic-slice_bitcast_fusion), channel_id=1, source_target_pairs={{0,4},{4,0},{1,5},{5,1},{2,6},{6,2},{3,7},{7,3},{8,12},{12,8},{9,1... | collective-permute-start | bytes 786440 | tf_op jit(solution)/shard_map/ppermute | solution.py:235
  (17 other events, 65.3 us)
Sparse Core Ops, SparseCore 0:
  89.8 62.5 reduce-scatter.2
  165.3 82.6 reduce-scatter.4
where the time goes:
time: 291 us; the launch traced here: 290 us
  waiting for transfers between devices  135 us (46%)
  starting transfers between devices  83.8 us (29%)
  Pallas kernels  43.9 us (15%)
  between operations  14.6 us (5%)
  local copies, waits for them, and re-layouts  7.13 us (2%)
  other arithmetic  5.66 us (2%)
    ppermute x28, waiting for transfers between devices, send(): return lax.ppermute(value, ('core', 'depth'), pairs)  85.3 us
    ppermute x28, starting transfers between devices, send(): return lax.ppermute(value, ('core', 'depth'), pairs)  57 us
    ppermute x15, waiting for transfers between devices, send(): lax.ppermute(value, 'chip', [(i, (i + sign) % chips) for i in range(chips)])  48.5 us
    pallas_call x3, Pallas kernels, sums_part(): pl.pallas_call(functools.partial(sums_kernel, units, sources), out_shape=...  28.3 us
    ppermute x15, starting transfers between devices, send(): lax.ppermute(value, 'chip', [(i, (i + sign) % chips) for i in range(chips)])  20 us
    pallas_call x2, Pallas kernels, warp_some(): pl.pallas_call(functools.partial(warp_kernel, depth, chunks), out_shape=[...  15.6 us
    ppermute x1, starting transfers between devices, per_device(): other = lax.ppermute(other, 'core', [(c, c ^ 1) for c in range(CORES)])  6.67 us
  transfers between devices with their start and end apart: 46, of which 28 were waited for; matrix products, arithmetic and copies ran while one was open for 1% of the time, Pallas kernels for 12%

commit v1 on v0

--- a/solution.py
+++ b/solution.py
@@ -190,25 +190,30 @@
         ]
         return lax.ppermute(value, ("core", "depth"), pairs)
 
+    sources = depth * CORES
+    order = [(k, h) for k in range(depth) for h in range(CORES)]
+
+    def warped(chunks):
+        return warp_some(visit_tiles, warp_matrix, flux_scale, where, depth, chunks)
+
+    def exchanged(pieces):
+        return [send(piece, k, h) for piece, (k, h) in zip(pieces, order)]
+
+    pieces = warped(CHUNKS[:1])
+    pieces, clip_bits = lax.optimization_barrier((pieces, clip_bits))
+    tiles = []
+    tiles.append(exchanged(pieces))
     words = clip_bits.reshape(entries, depth, CORES, half).transpose(1, 2, 0, 3)
     names = jnp.zeros((8, half), jnp.int32).at[0, :entries].set(patch_lists.reshape(entries))
     bits = []
-    for k in range(depth):
-        for h in range(CORES):
-            message = words[lax.rem(here + k, depth), core if h == 0 else 1 - core]
-            bits.append(jnp.concatenate([message, names]))
-    where, bits = lax.optimization_barrier((where, bits))
-    bits = [send(bits[k * CORES + h], k, h) for k in range(depth) for h in range(CORES)]
+    for k, h in order:
+        message = words[lax.rem(here + k, depth), core if h == 0 else 1 - core]
+        bits.append(jnp.concatenate([message, names]))
+    bits = exchanged(bits)
+    pieces = warped(CHUNKS[1:])
+    for n in range(1, len(CHUNKS)):
+        tiles.append(exchanged(pieces[(n - 1) * sources : n * sources]))
     patch_ids = jnp.stack([b[entries, :entries] for b in bits])
-
-    pieces = []
-    for chunks in (CHUNKS[:1], CHUNKS[1:]):
-        pieces += warp_some(visit_tiles, warp_matrix, flux_scale, where, depth, chunks)
-    sources = depth * CORES
-    tiles = []
-    for n in range(len(CHUNKS)):
-        mine = pieces[n * sources : (n + 1) * sources]
-        tiles.append([send(mine[k * CORES + h], k, h) for k in range(depth) for h in range(CORES)])
     totals = []
     for n, units in enumerate(CHUNKS):
         sums = sums_part(tiles[n], bits, patch_ids, patches, units)

time: 291 us -> 296 us (1.017)
  waiting for transfers between devices: 135 us -> 142 us
    ppermute x28, waiting for transfers between devices: 85.3 us -> 93.1 us  [send(): return lax.ppermute(value, ('core', 'depth'), pairs)]
  transfers between devices with their start and end apart: 46 -> 46, of which waited for: 28 -> 26; matrix products, arithmetic and copies ran while one was open for 1% -> 1% of each run, Pallas kernels for 12% -> 10%
where the time goes in v1:
time: 296 us; the launch traced here: 295 us
  waiting for transfers between devices  142 us (48%)
  starting transfers between devices  82.1 us (28%)
  Pallas kernels  44 us (15%)
  between operations  14.6 us (5%)
  other arithmetic  6.34 us (2%)
  local copies, waits for them, and re-layouts  5.76 us (2%)
    ppermute x28, waiting for transfers between devices, send(): return lax.ppermute(value, ('core', 'depth'), pairs)  93.1 us
    ppermute x28, starting transfers between devices, send(): return lax.ppermute(value, ('core', 'depth'), pairs)  54.7 us
    ppermute x15, waiting for transfers between devices, send(): lax.ppermute(value, 'chip', [(i, (i + sign) % chips) for i in range(chips)])  47.7 us
    pallas_call x3, Pallas kernels, sums_part(): pl.pallas_call(functools.partial(sums_kernel, units, sources), out_shape=...  28.3 us
    ppermute x15, starting transfers between devices, send(): lax.ppermute(value, 'chip', [(i, (i + sign) % chips) for i in range(chips)])  20.1 us
    pallas_call x2, Pallas kernels, warp_some(): pl.pallas_call(functools.partial(warp_kernel, depth, chunks), out_shape=[...  15.7 us
    ppermute x1, starting transfers between devices, per_device(): other = lax.ppermute(other, 'core', [(c, c ^ 1) for c in range(CORES)])  7.18 us
  transfers between devices with their start and end apart: 46, of which 26 were waited for; matrix products, arithmetic and copies ran while one was open for 1% of the time, Pallas kernels for 10%

profile of v1, /device:TPU:33, one launch (start us, length us, event | category | flops | bytes accessed | tf_op | source)
XLA Modules:
  0.0 295.1 jit_solution(10860893038850237419)
XLA Ops:
  7.3 0.8 slice.97
  8.7 6.8 %warp_some.2 = (bf16[128,8,128]{2,1,0:T(8,128)(2,1)}, bf16[128,8,128]{2,1,0:T(8,128)(2,1)}, bf16[128,8,128]{2,1,0:T(8,128)(2,1)}, bf16[128,8,128]{2,1,0:T(8,128)...) custom-call(s32[2]{0:T(128)} %pad_add_fusion.8.where_ref, ...), custom_call_target="tpu_custom_call" | custom-call | flops 4294967296 | bytes 16777216 | tf_op jit(solution)/shard_map/warp_some/pallas_call | solution.py:54
  15.4 0.9 reshape.525
  16.4 1.0 constant_dynamic-slice_fusion.1
  17.5 0.8 pad_add_fusion.7
  18.3 20.4 %collective-permute-start.2 = (s32[136,256]{1,0:T(8,128)S(1)}, s32[136,256]{1,0:T(8,128)S(1)}, u32[]{:S(2)}, u32[]{:S(2)}) collective-permute-start(s32[136,256]{1,0:T(8,128)S(1)} %get-tuple-element.216), channel_id=1, source_target_pairs={{0,4},{1,5},{2,6},{3,7},{4,0},{5,1},{6,2},{7,3},{8,12},{9,13},{10,... | collective-permute-start | bytes 417800 | tf_op jit(solution)/shard_map/ppermute | solution.py:191
  38.7 4.0 %collective-permute-start.5 = (s32[136,256]{1,0:T(8,128)S(1)}, s32[136,256]{1,0:T(8,128)S(1)}, u32[]{:S(2)}, u32[]{:S(2)}) collective-permute-start(s32[136,256]{1,0:T(8,128)S(1)} %get-tuple-element.219), channel_id=1, source_target_pairs={{0,2},{1,3},{2,0},{3,1},{4,6},{5,7},{6,4},{7,5},{8,10},{9,11},{10,... | collective-permute-start | bytes 417800 | tf_op jit(solution)/shard_map/ppermute | solution.py:191
  43.4 1.8 collective-permute-done.3.refs_10_
  45.1 6.6 %collective-permute-done.4.refs_11_ = s32[136,256]{1,0:T(8,128)S(1)} collective-permute-done((s32[136,256]{1,0:T(8,128)S(1)}, s32[136,256]{1,0:T(8,128)S(1)}, u32[]{:S(2)}, u32[]{:S(2)}) %collective-permute-start.4) | collective-permute-done | bytes 139296 | tf_op jit(solution)/shard_map/ppermute | solution.py:191
  51.9 6.5 %collective-permute-done.6.refs_13_ = s32[136,256]{1,0:T(8,128)S(1)} collective-permute-done((s32[136,256]{1,0:T(8,128)S(1)}, s32[136,256]{1,0:T(8,128)S(1)}, u32[]{:S(2)}, u32[]{:S(2)}) %collective-permute-start.6) | collective-permute-done | bytes 139296 | tf_op jit(solution)/shard_map/ppermute | solution.py:191
  58.4 2.1 collective-permute-start.12
  60.5 1.5 collective-permute-start.13
  61.9 2.9 collective-permute-start.14
  65.7 13.5 %collective-permute-done.11.refs_3_ = bf16[128,8,128]{2,1,0:T(8,128)(2,1)S(1)} collective-permute-done((bf16[128,8,128]{2,1,0:T(8,128)(2,1)}, bf16[128,8,128]{2,1,0:T(8,128)(2,1)S(1)}, u32[]{:S(2)}, u32[]{:S(2)}) %collective-permute-start.11) | collective-permute-done | bytes 262176 | tf_op jit(solution)/shard_map/ppermute | solution.py:191
  79.5 6.0 %collective-permute-done.15.refs_7_ = bf16[128,8,128]{2,1,0:T(8,128)(2,1)S(1)} collective-permute-done((bf16[128,8,128]{2,1,0:T(8,128)(2,1)S(1)}, bf16[128,8,128]{2,1,0:T(8,128)(2,1)S(1)}, u32[]{:S(2)}, u32[]{:S(2)}) %collective-permute-start.15) | collective-permute-done | bytes 262176 | tf_op jit(solution)/shard_map/ppermute | solution.py:191
  86.2 8.5 %sums_part.3 = f32[128,5,8,128]{3,2,1,0:T(8,128)} custom-call(s32[8,128]{1,0:T(8,128)} %stack.17.patch_ref, bf16[128,8,128]{2,1,0:T(8,128)(2,1)} %get-tuple-element.151.refs_0_, bf16[128,8,128]{2,1,0:T(8,128)(2,1)} %copy-done.14, bf16[128,8,128]{2,1,0:T(8,128)(2,1)} %copy-done.15, bf16[128,8,128]{2,1,0:T(8,128)(2,1)} %copy-done.22, ...), custom_call_target="tpu_custom_call" | custom-call | flops 52428800 | bytes 2621440 | tf_op jit(solution)/shard_map/sums_part/pallas_call | solution.py:126
  94.8 8.9 %warp_some.3 = (bf16[128,16,128]{2,1,0:T(8,128)(2,1)}, bf16[128,16,128]{2,1,0:T(8,128)(2,1)}, bf16[128,16,128]{2,1,0:T(8,128)(2,1)}, bf16[128,16,128]{2,1,0:T(8,...) custom-call(s32[2]{0:T(128)} %pad_add_fusion.8.where_ref, ...), custom_call_target="tpu_custom_call" | custom-call | flops 4294967296 | bytes 16777216 | tf_op jit(solution)/shard_map/warp_some/pallas_call | solution.py:54
  103.8 2.0 collective-permute-start.17
  106.2 2.1 collective-permute-start.19
  108.3 1.0 collective-permute-start.20
  109.4 2.6 collective-permute-start.21
  112.1 6.8 %collective-permute-done.17.refs_2_ = bf16[128,16,128]{2,1,0:T(8,128)(2,1)S(1)} collective-permute-done((bf16[128,16,128]{2,1,0:T(8,128)(2,1)}, bf16[128,16,128]{2,1,0:T(8,128)(2,1)S(1)}, u32[]{:S(2)}, u32[]{:S(2)}) %collective-permute-start.17) | collective-permute-done | bytes 524320 | tf_op jit(solution)/shard_map/ppermute | solution.py:191
  118.8 3.0 %collective-permute-start.22 = (bf16[128,16,128]{2,1,0:T(8,128)(2,1)}, bf16[128,16,128]{2,1,0:T(8,128)(2,1)}, u32[]{:S(2)}, u32[]{:S(2)}) collective-permute-start(bf16[128,16,128]{2,1,0:T(8,128)(2,1)} %get-tuple-element.166), channel_id=1, source_target_pairs={{0,7},{1,4},{2,5},{3,6},{4,3},{5,0},{6,1},{7,2},{8,15},{9,12},{10,... | collective-permute-start | bytes 1572872 | tf_op jit(solution)/shard_map/ppermute | solution.py:191
  121.8 9.0 %collective-permute-done.18.refs_3_ = bf16[128,16,128]{2,1,0:T(8,128)(2,1)S(1)} collective-permute-done((bf16[128,16,128]{2,1,0:T(8,128)(2,1)}, bf16[128,16,128]{2,1,0:T(8,128)(2,1)S(1)}, u32[]{:S(2)}, u32[]{:S(2)}) %collective-permute-start.18) | collective-permute-done | bytes 524320 | tf_op jit(solution)/shard_map/ppermute | solution.py:191
  130.8 11.7 %collective-permute-done.19.refs_4_ = bf16[128,16,128]{2,1,0:T(8,128)(2,1)S(1)} collective-permute-done((bf16[128,16,128]{2,1,0:T(8,128)(2,1)}, bf16[128,16,128]{2,1,0:T(8,128)(2,1)S(1)}, u32[]{:S(2)}, u32[]{:S(2)}) %collective-permute-start.19) | collective-permute-done | bytes 524320 | tf_op jit(solution)/shard_map/ppermute | solution.py:191
  142.5 11.5 %collective-permute-done.20.refs_5_ = bf16[128,16,128]{2,1,0:T(8,128)(2,1)S(1)} collective-permute-done((bf16[128,16,128]{2,1,0:T(8,128)(2,1)}, bf16[128,16,128]{2,1,0:T(8,128)(2,1)S(1)}, u32[]{:S(2)}, u32[]{:S(2)}) %collective-permute-start.20) | collective-permute-done | bytes 524320 | tf_op jit(solution)/shard_map/ppermute | solution.py:191
  154.1 1.9 collective-permute-done.22.refs_7_
  156.0 12.9 %sums_part.4 = f32[128,5,16,128]{3,2,1,0:T(8,128)} custom-call(s32[8,128]{1,0:T(8,128)} %stack.17.patch_ref, bf16[128,16,128]{2,1,0:T(8,128)(2,1)} %get-tuple-element.159.refs_0_, bf16[128,16,128]{2,1,0:T(8,128)(2,1)} %copy-done.8, bf16[128,16,128]{2,1,0:T(8,128)(2,1)} %copy-done.9, bf16[128,16,128]{2,1,0:T(8,128)(2,1)} %copy-done.10, ...), custom_call_target="tpu_custom_call" | custom-call | flops 104857600 | bytes 5242880 | tf_op jit(solution)/shard_map/sums_part/pallas_call | solution.py:126
  169.0 0.8 copy-done.38
  169.9 1.8 collective-permute-start.24
  172.2 2.1 collective-permute-start.26
  174.3 1.0 collective-permute-start.27
  175.3 2.9 collective-permute-start.28
  178.5 3.2 %collective-permute-start.29 = (bf16[128,8,128]{2,1,0:T(8,128)(2,1)S(1)}, bf16[128,8,128]{2,1,0:T(8,128)(2,1)S(1)}, u32[]{:S(2)}, u32[]{:S(2)}) collective-permute-start(bf16[128,8,128]{2,1,0:T(8,128)(2,1)S(1)} %copy-done.32), channel_id=1, source_target_pairs={{0,7},{1,4},{2,5},{3,6},{4,3},{5,0},{6,1},{7,2},{8,15},{9,12},{10,... | collective-permute-start | bytes 786440 | tf_op jit(solution)/shard_map/ppermute | solution.py:191
  181.7 3.0 %collective-permute-done.25.refs_3_ = bf16[128,8,128]{2,1,0:T(8,128)(2,1)S(1)} collective-permute-done((bf16[128,8,128]{2,1,0:T(8,128)(2,1)S(1)}, bf16[128,8,128]{2,1,0:T(8,128)(2,1)S(1)}, u32[]{:S(2)}, u32[]{:S(2)}) %collective-permute-start.25) | collective-permute-done | bytes 262176 | tf_op jit(solution)/shard_map/ppermute | solution.py:191
  184.7 6.5 %collective-permute-done.26.refs_4_ = bf16[128,8,128]{2,1,0:T(8,128)(2,1)S(1)} collective-permute-done((bf16[128,8,128]{2,1,0:T(8,128)(2,1)S(1)}, bf16[128,8,128]{2,1,0:T(8,128)(2,1)S(1)}, u32[]{:S(2)}, u32[]{:S(2)}) %collective-permute-start.26) | collective-permute-done | bytes 262176 | tf_op jit(solution)/shard_map/ppermute | solution.py:191
  191.2 5.9 %collective-permute-done.27.refs_5_ = bf16[128,8,128]{2,1,0:T(8,128)(2,1)S(1)} collective-permute-done((bf16[128,8,128]{2,1,0:T(8,128)(2,1)S(1)}, bf16[128,8,128]{2,1,0:T(8,128)(2,1)S(1)}, u32[]{:S(2)}, u32[]{:S(2)}) %collective-permute-start.27) | collective-permute-done | bytes 262176 | tf_op jit(solution)/shard_map/ppermute | solution.py:191
  197.1 1.9 collective-permute-done.29.refs_7_
  199.1 0.7 copy-done.23
  199.8 7.0 %sums_part.5 = f32[128,5,8,128]{3,2,1,0:T(8,128)S(1)} custom-call(s32[8,128]{1,0:T(8,128)} %stack.17.patch_ref, bf16[128,8,128]{2,1,0:T(8,128)(2,1)} %get-tuple-element.167.refs_0_, bf16[128,8,128]{2,1,0:T(8,128)(2,1)} %copy-done.16, bf16[128,8,128]{2,1,0:T(8,128)(2,1)} %copy-done.17, bf16[128,8,128]{2,1,0:T(8,128)(2,1)} %copy-done.18, ...), custom_call_target="tpu_custom_call" | custom-call | flops 52428800 | bytes 2621440 | tf_op jit(solution)/shard_map/sums_part/pallas_call | solution.py:126
  207.0 14.1 %collective-permute-done.30 = f32[8,5,8,128]{3,2,1,0:T(8,128)S(1)} collective-permute-done((f32[8,5,8,128]{3,2,1,0:T(8,128)S(1)}, f32[8,5,8,128]{3,2,1,0:T(8,128)S(1)}, u32[]{:S(2)}, u32[]{:S(2)}) %collective-permute-start.30) | collective-permute-done | bytes 163872 | tf_op jit(solution)/shard_map/ppermute | solution.py:148
  221.1 53.9 %while.16 = (s32[]{:T(128)}, f32[8,5,8,128]{3,2,1,0:T(8,128)S(1)}, f32[8,5,8,128]{3,2,1,0:T(8,128)S(1)}, s32[]{:T(128)}, f32[128,5,8,128]{3,2,1,0:T(8,128)S(1)},...) while((s32[]{:T(128)}, f32[8,5,8,128]{3,2,1,0:T(8,128)S(1)}, ...), condition=%wide.region_3.0_spmd, body=%wide.region_2.0_spmd.sunk | while | flops 81948 | bytes 2294243 | solution.py:156
  221.3 2.6 collective-permute-start.1
  224.0 8.0 %collective-permute-done = f32[8,5,8,128]{3,2,1,0:T(8,128)S(1)} collective-permute-done((f32[8,5,8,128]{3,2,1,0:T(8,128)S(1)}, f32[8,5,8,128]{3,2,1,0:T(8,128)S(1)}, u32[]{:S(2)}, u32[]{:S(2)}) %collective-permute-start) | collective-permute-done | bytes 163872 | tf_op jit(solution)/shard_map/while/body/eval_jaxpr/ppermute | solution.py:148
  232.2 2.6 collective-permute-start.1
  234.8 7.5 %collective-permute-done = f32[8,5,8,128]{3,2,1,0:T(8,128)S(1)} collective-permute-done((f32[8,5,8,128]{3,2,1,0:T(8,128)S(1)}, f32[8,5,8,128]{3,2,1,0:T(8,128)S(1)}, u32[]{:S(2)}, u32[]{:S(2)}) %collective-permute-start) | collective-permute-done | bytes 163872 | tf_op jit(solution)/shard_map/while/body/eval_jaxpr/ppermute | solution.py:148
  242.6 2.8 collective-permute-start.1
  245.3 6.3 %collective-permute-done = f32[8,5,8,128]{3,2,1,0:T(8,128)S(1)} collective-permute-done((f32[8,5,8,128]{3,2,1,0:T(8,128)S(1)}, f32[8,5,8,128]{3,2,1,0:T(8,128)S(1)}, u32[]{:S(2)}, u32[]{:S(2)}) %collective-permute-start) | collective-permute-done | bytes 163872 | tf_op jit(solution)/shard_map/while/body/eval_jaxpr/ppermute | solution.py:148
  252.0 2.6 collective-permute-start.1
  254.6 3.1 %collective-permute-done = f32[8,5,8,128]{3,2,1,0:T(8,128)S(1)} collective-permute-done((f32[8,5,8,128]{3,2,1,0:T(8,128)S(1)}, f32[8,5,8,128]{3,2,1,0:T(8,128)S(1)}, u32[]{:S(2)}, u32[]{:S(2)}) %collective-permute-start) | collective-permute-done | bytes 163872 | tf_op jit(solution)/shard_map/while/body/eval_jaxpr/ppermute | solution.py:148
  257.8 0.8 collective-permute-start
  258.6 2.0 collective-permute-start.1
  260.6 2.7 collective-permute-done
  263.5 2.8 collective-permute-start.1
  266.3 2.6 collective-permute-done
  269.1 2.9 collective-permute-start.1
  272.0 3.0 %collective-permute-done = f32[8,5,8,128]{3,2,1,0:T(8,128)S(1)} collective-permute-done((f32[8,5,8,128]{3,2,1,0:T(8,128)S(1)}, f32[8,5,8,128]{3,2,1,0:T(8,128)S(1)}, u32[]{:S(2)}, u32[]{:S(2)}) %collective-permute-start) | collective-permute-done | bytes 163872 | tf_op jit(solution)/shard_map/while/body/eval_jaxpr/ppermute | solution.py:148
  275.1 0.8 divide_add_fusion.2
  276.0 0.9 fusion.13
  276.9 1.0 divide_add_fusion
  277.8 1.0 fusion.4
  279.0 7.2 %collective-permute-start.31 = (f32[4,4,16,256]{3,2,1,0:T(8,128)S(1)}, f32[4,4,16,256]{3,2,1,0:T(8,128)S(1)}, u32[]{:S(2)}, u32[]{:S(2)}) collective-permute-start(f32[4,4,16,256]{3,2,1,0:T(8,128)S(1)} %dynamic-slice_bitcast_fusion), channel_id=1, source_target_pairs={{0,4},{4,0},{1,5},{5,1},{2,6},{6,2},{3,7},{7,3},{8,12},{12,8},{9,1... | collective-permute-start | bytes 786440 | tf_op jit(solution)/shard_map/ppermute | solution.py:240
  286.2 1.2 collective-permute-done.31
  287.4 0.9 pad_maximum_fusion
  (153 shorter events, 6.6 us)
Async XLA Ops:
  7.2 268.0 %reduce-scatter.3.cloned.1.call-start = ((), (), s32[]{:S(2)}) async-start(), calls=%async_computation.2 | async-start | bytes 2785280 | tf_op jit(solution)/shard_map/reduce_scatter | solution.py:222
  17.3 25.4 %copy-start.31 = (bf16[128,8,128]{2,1,0:T(8,128)(2,1)S(1)}, bf16[128,8,128]{2,1,0:T(8,128)(2,1)}, u32[]{:S(2)}) copy-start(bf16[128,8,128]{2,1,0:T(8,128)(2,1)} %get-tuple-element.152) | copy-start | bytes 786436
  17.4 25.9 %copy-start.30 = (bf16[128,8,128]{2,1,0:T(8,128)(2,1)S(1)}, bf16[128,8,128]{2,1,0:T(8,128)(2,1)}, u32[]{:S(2)}) copy-start(bf16[128,8,128]{2,1,0:T(8,128)(2,1)} %get-tuple-element.153) | copy-start | bytes 786436
  17.4 44.6 %copy-start.29 = (bf16[128,8,128]{2,1,0:T(8,128)(2,1)S(1)}, bf16[128,8,128]{2,1,0:T(8,128)(2,1)}, u32[]{:S(2)}) copy-start(bf16[128,8,128]{2,1,0:T(8,128)(2,1)} %get-tuple-element.157) | copy-start | bytes 786436
  17.4 47.5 %copy-start.28 = (bf16[128,8,128]{2,1,0:T(8,128)(2,1)S(1)}, bf16[128,8,128]{2,1,0:T(8,128)(2,1)}, u32[]{:S(2)}) copy-start(bf16[128,8,128]{2,1,0:T(8,128)(2,1)} %get-tuple-element.158) | copy-start | bytes 786436
  18.3 25.0 %collective-permute-start.2 = (s32[136,256]{1,0:T(8,128)S(1)}, s32[136,256]{1,0:T(8,128)S(1)}, u32[]{:S(2)}, u32[]{:S(2)}) collective-permute-start(s32[136,256]{1,0:T(8,128)S(1)} %get-tuple-element.216), channel_id=1, source_target_pairs={{0,4},{1,5},{2,6},{3,7},{4,0},{5,1},{6,2},{7,3},{8,12},{9,13},{10,... | collective-permute-start | bytes 417800 | tf_op jit(solution)/shard_map/ppermute | solution.py:191
  38.7 6.4 %collective-permute-start.3 = (s32[136,256]{1,0:T(8,128)S(1)}, s32[136,256]{1,0:T(8,128)S(1)}, u32[]{:S(2)}, u32[]{:S(2)}) collective-permute-start(s32[136,256]{1,0:T(8,128)S(1)} %get-tuple-element.217), channel_id=1, source_target_pairs={{0,1},{1,2},{2,3},{3,0},{4,5},{5,6},{6,7},{7,4},{8,9},{9,10},{10,1... | collective-permute-start | bytes 417800 | tf_op jit(solution)/shard_map/ppermute | solution.py:191
  38.7 13.0 %collective-permute-start.4 = (s32[136,256]{1,0:T(8,128)S(1)}, s32[136,256]{1,0:T(8,128)S(1)}, u32[]{:S(2)}, u32[]{:S(2)}) collective-permute-start(s32[136,256]{1,0:T(8,128)S(1)} %get-tuple-element.218), channel_id=1, source_target_pairs={{0,5},{1,6},{2,7},{3,4},{4,1},{5,2},{6,3},{7,0},{8,13},{9,14},{10,... | collective-permute-start | bytes 417800 | tf_op jit(solution)/shard_map/ppermute | solution.py:191
  38.7 13.0 %collective-permute-start.5 = (s32[136,256]{1,0:T(8,128)S(1)}, s32[136,256]{1,0:T(8,128)S(1)}, u32[]{:S(2)}, u32[]{:S(2)}) collective-permute-start(s32[136,256]{1,0:T(8,128)S(1)} %get-tuple-element.219), channel_id=1, source_target_pairs={{0,2},{1,3},{2,0},{3,1},{4,6},{5,7},{6,4},{7,5},{8,10},{9,11},{10,... | collective-permute-start | bytes 417800 | tf_op jit(solution)/shard_map/ppermute | solution.py:191
  42.7 19.2 %collective-permute-start.9 = (bf16[128,8,128]{2,1,0:T(8,128)(2,1)S(1)}, bf16[128,8,128]{2,1,0:T(8,128)(2,1)S(1)}, u32[]{:S(2)}, u32[]{:S(2)}) collective-permute-start(bf16[128,8,128]{2,1,0:T(8,128)(2,1)S(1)} %copy-done.31), channel_id=1, source_target_pairs={{0,4},{1,5},{2,6},{3,7},{4,0},{5,1},{6,2},{7,3},{8,12},{9,13},{10,... | collective-permute-start | bytes 786440 | tf_op jit(solution)/shard_map/ppermute | solution.py:191
  43.2 42.3 %copy-start = (s32[136,256]{1,0:T(8,128)}, s32[136,256]{1,0:T(8,128)S(1)}, u32[]{:S(2)}) copy-start(s32[136,256]{1,0:T(8,128)S(1)} %collective-permute-done.2.refs_9_) | copy-start | bytes 417796
  43.2 21.7 %collective-permute-start.10 = (bf16[128,8,128]{2,1,0:T(8,128)(2,1)S(1)}, bf16[128,8,128]{2,1,0:T(8,128)(2,1)S(1)}, u32[]{:S(2)}, u32[]{:S(2)}) collective-permute-start(bf16[128,8,128]{2,1,0:T(8,128)(2,1)S(1)} %copy-done.30), channel_id=1, source_target_pairs={{0,1},{1,2},{2,3},{3,0},{4,5},{5,6},{6,7},{7,4},{8,9},{9,10},{10,1... | collective-permute-start | bytes 786440 | tf_op jit(solution)/shard_map/ppermute | solution.py:191
  45.1 40.4 %copy-start.1 = (s32[136,256]{1,0:T(8,128)}, s32[136,256]{1,0:T(8,128)S(1)}, u32[]{:S(2)}) copy-start(s32[136,256]{1,0:T(8,128)S(1)} %collective-permute-done.3.refs_10_) | copy-start | bytes 417796
  45.1 13.3 %collective-permute-start.6 = (s32[136,256]{1,0:T(8,128)S(1)}, s32[136,256]{1,0:T(8,128)S(1)}, u32[]{:S(2)}, u32[]{:S(2)}) collective-permute-start(s32[136,256]{1,0:T(8,128)S(1)} %get-tuple-element.220), channel_id=1, source_target_pairs={{0,6},{1,7},{2,4},{3,5},{4,2},{5,3},{6,0},{7,1},{8,14},{9,15},{10,... | collective-permute-start | bytes 417800 | tf_op jit(solution)/shard_map/ppermute | solution.py:191
  51.7 33.8 %copy-start.2 = (s32[136,256]{1,0:T(8,128)}, s32[136,256]{1,0:T(8,128)S(1)}, u32[]{:S(2)}) copy-start(s32[136,256]{1,0:T(8,128)S(1)} %collective-permute-done.4.refs_11_) | copy-start | bytes 417796
  51.7 6.7 %collective-permute-start.7 = (s32[136,256]{1,0:T(8,128)S(1)}, s32[136,256]{1,0:T(8,128)S(1)}, u32[]{:S(2)}, u32[]{:S(2)}) collective-permute-start(s32[136,256]{1,0:T(8,128)S(1)} %get-tuple-element.221), channel_id=1, source_target_pairs={{0,3},{1,0},{2,1},{3,2},{4,7},{5,4},{6,5},{7,6},{8,11},{9,8},{10,9... | collective-permute-start | bytes 417800 | tf_op jit(solution)/shard_map/ppermute | solution.py:191
  51.7 33.8 %copy-start.3 = (s32[136,256]{1,0:T(8,128)}, s32[136,256]{1,0:T(8,128)S(1)}, u32[]{:S(2)}) copy-start(s32[136,256]{1,0:T(8,128)S(1)} %collective-permute-done.5.refs_12_) | copy-start | bytes 417796
  51.7 8.7 %collective-permute-start.8 = (s32[136,256]{1,0:T(8,128)S(1)}, s32[136,256]{1,0:T(8,128)S(1)}, u32[]{:S(2)}, u32[]{:S(2)}) collective-permute-start(s32[136,256]{1,0:T(8,128)S(1)} %get-tuple-element.222), channel_id=1, source_target_pairs={{0,7},{1,4},{2,5},{3,6},{4,3},{5,0},{6,1},{7,2},{8,15},{9,12},{10,... | collective-permute-start | bytes 417800 | tf_op jit(solution)/shard_map/ppermute | solution.py:191
  58.4 27.1 %copy-start.4 = (s32[136,256]{1,0:T(8,128)}, s32[136,256]{1,0:T(8,128)S(1)}, u32[]{:S(2)}) copy-start(s32[136,256]{1,0:T(8,128)S(1)} %collective-permute-done.6.refs_13_) | copy-start | bytes 417796
  58.4 20.9 %collective-permute-start.11 = (bf16[128,8,128]{2,1,0:T(8,128)(2,1)}, bf16[128,8,128]{2,1,0:T(8,128)(2,1)S(1)}, u32[]{:S(2)}, u32[]{:S(2)}) collective-permute-start(bf16[128,8,128]{2,1,0:T(8,128)(2,1)} %get-tuple-element.154), channel_id=1, source_target_pairs={{0,5},{1,6},{2,7},{3,4},{4,1},{5,2},{6,3},{7,0},{8,13},{9,14},{10,... | collective-permute-start | bytes 786440 | tf_op jit(solution)/shard_map/ppermute | solution.py:191
  58.4 27.1 %copy-start.5 = (s32[136,256]{1,0:T(8,128)}, s32[136,256]{1,0:T(8,128)S(1)}, u32[]{:S(2)}) copy-start(s32[136,256]{1,0:T(8,128)S(1)} %collective-permute-done.7.refs_14_) | copy-start | bytes 417796
  58.4 20.8 %collective-permute-start.12 = (bf16[128,8,128]{2,1,0:T(8,128)(2,1)}, bf16[128,8,128]{2,1,0:T(8,128)(2,1)S(1)}, u32[]{:S(2)}, u32[]{:S(2)}) collective-permute-start(bf16[128,8,128]{2,1,0:T(8,128)(2,1)} %get-tuple-element.155), channel_id=1, source_target_pairs={{0,2},{1,3},{2,0},{3,1},{4,6},{5,7},{6,4},{7,5},{8,10},{9,11},{10,... | collective-permute-start | bytes 786440 | tf_op jit(solution)/shard_map/ppermute | solution.py:191
  60.5 25.1 %copy-start.6 = (s32[136,256]{1,0:T(8,128)}, s32[136,256]{1,0:T(8,128)S(1)}, u32[]{:S(2)}) copy-start(s32[136,256]{1,0:T(8,128)S(1)} %collective-permute-done.8.refs_15_) | copy-start | bytes 417796
  60.5 18.8 %collective-permute-start.13 = (bf16[128,8,128]{2,1,0:T(8,128)(2,1)}, bf16[128,8,128]{2,1,0:T(8,128)(2,1)S(1)}, u32[]{:S(2)}, u32[]{:S(2)}) collective-permute-start(bf16[128,8,128]{2,1,0:T(8,128)(2,1)} %get-tuple-element.156), channel_id=1, source_target_pairs={{0,6},{1,7},{2,4},{3,5},{4,2},{5,3},{6,0},{7,1},{8,14},{9,15},{10,... | collective-permute-start | bytes 786440 | tf_op jit(solution)/shard_map/ppermute | solution.py:191
  61.9 23.6 %copy-start.14 = (bf16[128,8,128]{2,1,0:T(8,128)(2,1)}, bf16[128,8,128]{2,1,0:T(8,128)(2,1)S(1)}, u32[]{:S(2)}) copy-start(bf16[128,8,128]{2,1,0:T(8,128)(2,1)S(1)} %collective-permute-done.9.refs_1_) | copy-start | bytes 786436
  61.9 17.5 %collective-permute-start.14 = (bf16[128,8,128]{2,1,0:T(8,128)(2,1)S(1)}, bf16[128,8,128]{2,1,0:T(8,128)(2,1)S(1)}, u32[]{:S(2)}, u32[]{:S(2)}) collective-permute-start(bf16[128,8,128]{2,1,0:T(8,128)(2,1)S(1)} %copy-done.29), channel_id=1, source_target_pairs={{0,3},{1,0},{2,1},{3,2},{4,7},{5,4},{6,5},{7,6},{8,11},{9,8},{10,9... | collective-permute-start | bytes 786440 | tf_op jit(solution)/shard_map/ppermute | solution.py:191
  64.9 20.6 %copy-start.15 = (bf16[128,8,128]{2,1,0:T(8,128)(2,1)}, bf16[128,8,128]{2,1,0:T(8,128)(2,1)S(1)}, u32[]{:S(2)}) copy-start(bf16[128,8,128]{2,1,0:T(8,128)(2,1)S(1)} %collective-permute-done.10.refs_2_) | copy-start | bytes 786436
  64.9 20.6 %collective-permute-start.15 = (bf16[128,8,128]{2,1,0:T(8,128)(2,1)S(1)}, bf16[128,8,128]{2,1,0:T(8,128)(2,1)S(1)}, u32[]{:S(2)}, u32[]{:S(2)}) collective-permute-start(bf16[128,8,128]{2,1,0:T(8,128)(2,1)S(1)} %copy-done.28), channel_id=1, source_target_pairs={{0,7},{1,4},{2,5},{3,6},{4,3},{5,0},{6,1},{7,2},{8,15},{9,12},{10,... | collective-permute-start | bytes 786440 | tf_op jit(solution)/shard_map/ppermute | solution.py:191
  94.7 182.1 %reduce-scatter.5.cloned.1.call-start = ((), (), s32[]{:S(2)}) async-start(), calls=%async_computation.3 | async-start | bytes 5570560 | tf_op jit(solution)/shard_map/reduce_scatter | solution.py:222
  103.7 5.7 %collective-permute-start.16 = (bf16[128,16,128]{2,1,0:T(8,128)(2,1)}, bf16[128,16,128]{2,1,0:T(8,128)(2,1)S(1)}, u32[]{:S(2)}, u32[]{:S(2)}) collective-permute-start(bf16[128,16,128]{2,1,0:T(8,128)(2,1)} %get-tuple-element.160), channel_id=1, source_target_pairs={{0,4},{1,5},{2,6},{3,7},{4,0},{5,1},{6,2},{7,3},{8,12},{9,13},{10,... | collective-permute-start | bytes 1572872 | tf_op jit(solution)/shard_map/ppermute | solution.py:191
  103.8 15.0 %collective-permute-start.17 = (bf16[128,16,128]{2,1,0:T(8,128)(2,1)}, bf16[128,16,128]{2,1,0:T(8,128)(2,1)S(1)}, u32[]{:S(2)}, u32[]{:S(2)}) collective-permute-start(bf16[128,16,128]{2,1,0:T(8,128)(2,1)} %get-tuple-element.161), channel_id=1, source_target_pairs={{0,1},{1,2},{2,3},{3,0},{4,5},{5,6},{6,7},{7,4},{8,9},{9,10},{10,1... | collective-permute-start | bytes 1572872 | tf_op jit(solution)/shard_map/ppermute | solution.py:191
  105.8 25.0 %collective-permute-start.18 = (bf16[128,16,128]{2,1,0:T(8,128)(2,1)}, bf16[128,16,128]{2,1,0:T(8,128)(2,1)S(1)}, u32[]{:S(2)}, u32[]{:S(2)}) collective-permute-start(bf16[128,16,128]{2,1,0:T(8,128)(2,1)} %get-tuple-element.162), channel_id=1, source_target_pairs={{0,5},{1,6},{2,7},{3,4},{4,1},{5,2},{6,3},{7,0},{8,13},{9,14},{10,... | collective-permute-start | bytes 1572872 | tf_op jit(solution)/shard_map/ppermute | solution.py:191
  106.2 36.3 %collective-permute-start.19 = (bf16[128,16,128]{2,1,0:T(8,128)(2,1)}, bf16[128,16,128]{2,1,0:T(8,128)(2,1)S(1)}, u32[]{:S(2)}, u32[]{:S(2)}) collective-permute-start(bf16[128,16,128]{2,1,0:T(8,128)(2,1)} %get-tuple-element.163), channel_id=1, source_target_pairs={{0,2},{1,3},{2,0},{3,1},{4,6},{5,7},{6,4},{7,5},{8,10},{9,11},{10,... | collective-permute-start | bytes 1572872 | tf_op jit(solution)/shard_map/ppermute | solution.py:191
  108.3 45.7 %collective-permute-start.20 = (bf16[128,16,128]{2,1,0:T(8,128)(2,1)}, bf16[128,16,128]{2,1,0:T(8,128)(2,1)S(1)}, u32[]{:S(2)}, u32[]{:S(2)}) collective-permute-start(bf16[128,16,128]{2,1,0:T(8,128)(2,1)} %get-tuple-element.164), channel_id=1, source_target_pairs={{0,6},{1,7},{2,4},{3,5},{4,2},{5,3},{6,0},{7,1},{8,14},{9,15},{10,... | collective-permute-start | bytes 1572872 | tf_op jit(solution)/shard_map/ppermute | solution.py:191
  109.4 46.5 %copy-start.8 = (bf16[128,16,128]{2,1,0:T(8,128)(2,1)}, bf16[128,16,128]{2,1,0:T(8,128)(2,1)S(1)}, u32[]{:S(2)}) copy-start(bf16[128,16,128]{2,1,0:T(8,128)(2,1)S(1)} %collective-permute-done.16.refs_1_) | copy-start | bytes 1572868
  109.4 44.7 %collective-permute-start.21 = (bf16[128,16,128]{2,1,0:T(8,128)(2,1)}, bf16[128,16,128]{2,1,0:T(8,128)(2,1)S(1)}, u32[]{:S(2)}, u32[]{:S(2)}) collective-permute-start(bf16[128,16,128]{2,1,0:T(8,128)(2,1)} %get-tuple-element.165), channel_id=1, source_target_pairs={{0,3},{1,0},{2,1},{3,2},{4,7},{5,4},{6,5},{7,6},{8,11},{9,8},{10,9... | collective-permute-start | bytes 1572872 | tf_op jit(solution)/shard_map/ppermute | solution.py:191
  118.8 37.1 %copy-start.9 = (bf16[128,16,128]{2,1,0:T(8,128)(2,1)}, bf16[128,16,128]{2,1,0:T(8,128)(2,1)S(1)}, u32[]{:S(2)}) copy-start(bf16[128,16,128]{2,1,0:T(8,128)(2,1)S(1)} %collective-permute-done.17.refs_2_) | copy-start | bytes 1572868
  118.8 37.1 %collective-permute-start.22 = (bf16[128,16,128]{2,1,0:T(8,128)(2,1)}, bf16[128,16,128]{2,1,0:T(8,128)(2,1)}, u32[]{:S(2)}, u32[]{:S(2)}) collective-permute-start(bf16[128,16,128]{2,1,0:T(8,128)(2,1)} %get-tuple-element.166), channel_id=1, source_target_pairs={{0,7},{1,4},{2,5},{3,6},{4,3},{5,0},{6,1},{7,2},{8,15},{9,12},{10,... | collective-permute-start | bytes 1572872 | tf_op jit(solution)/shard_map/ppermute | solution.py:191
  130.8 25.1 %copy-start.10 = (bf16[128,16,128]{2,1,0:T(8,128)(2,1)}, bf16[128,16,128]{2,1,0:T(8,128)(2,1)S(1)}, u32[]{:S(2)}) copy-start(bf16[128,16,128]{2,1,0:T(8,128)(2,1)S(1)} %collective-permute-done.18.refs_3_) | copy-start | bytes 1572868
  169.8 5.5 %collective-permute-start.23 = (bf16[128,8,128]{2,1,0:T(8,128)(2,1)S(1)}, bf16[128,8,128]{2,1,0:T(8,128)(2,1)S(1)}, u32[]{:S(2)}, u32[]{:S(2)}) collective-permute-start(bf16[128,8,128]{2,1,0:T(8,128)(2,1)S(1)} %copy-done.38), channel_id=1, source_target_pairs={{0,4},{1,5},{2,6},{3,7},{4,0},{5,1},{6,2},{7,3},{8,12},{9,13},{10,... | collective-permute-start | bytes 786440 | tf_op jit(solution)/shard_map/ppermute | solution.py:191
  169.9 8.6 %collective-permute-start.24 = (bf16[128,8,128]{2,1,0:T(8,128)(2,1)S(1)}, bf16[128,8,128]{2,1,0:T(8,128)(2,1)S(1)}, u32[]{:S(2)}, u32[]{:S(2)}) collective-permute-start(bf16[128,8,128]{2,1,0:T(8,128)(2,1)S(1)} %copy-done.37), channel_id=1, source_target_pairs={{0,1},{1,2},{2,3},{3,0},{4,5},{5,6},{6,7},{7,4},{8,9},{9,10},{10,1... | collective-permute-start | bytes 786440 | tf_op jit(solution)/shard_map/ppermute | solution.py:191
  171.7 13.1 %collective-permute-start.25 = (bf16[128,8,128]{2,1,0:T(8,128)(2,1)S(1)}, bf16[128,8,128]{2,1,0:T(8,128)(2,1)S(1)}, u32[]{:S(2)}, u32[]{:S(2)}) collective-permute-start(bf16[128,8,128]{2,1,0:T(8,128)(2,1)S(1)} %copy-done.36), channel_id=1, source_target_pairs={{0,5},{1,6},{2,7},{3,4},{4,1},{5,2},{6,3},{7,0},{8,13},{9,14},{10,... | collective-permute-start | bytes 786440 | tf_op jit(solution)/shard_map/ppermute | solution.py:191
  172.2 19.0 %collective-permute-start.26 = (bf16[128,8,128]{2,1,0:T(8,128)(2,1)S(1)}, bf16[128,8,128]{2,1,0:T(8,128)(2,1)S(1)}, u32[]{:S(2)}, u32[]{:S(2)}) collective-permute-start(bf16[128,8,128]{2,1,0:T(8,128)(2,1)S(1)} %copy-done.35), channel_id=1, source_target_pairs={{0,2},{1,3},{2,0},{3,1},{4,6},{5,7},{6,4},{7,5},{8,10},{9,11},{10,... | collective-permute-start | bytes 786440 | tf_op jit(solution)/shard_map/ppermute | solution.py:191
  174.3 22.8 %collective-permute-start.27 = (bf16[128,8,128]{2,1,0:T(8,128)(2,1)S(1)}, bf16[128,8,128]{2,1,0:T(8,128)(2,1)S(1)}, u32[]{:S(2)}, u32[]{:S(2)}) collective-permute-start(bf16[128,8,128]{2,1,0:T(8,128)(2,1)S(1)} %copy-done.34), channel_id=1, source_target_pairs={{0,6},{1,7},{2,4},{3,5},{4,2},{5,3},{6,0},{7,1},{8,14},{9,15},{10,... | collective-permute-start | bytes 786440 | tf_op jit(solution)/shard_map/ppermute | solution.py:191
  175.3 24.5 %copy-start.16 = (bf16[128,8,128]{2,1,0:T(8,128)(2,1)}, bf16[128,8,128]{2,1,0:T(8,128)(2,1)S(1)}, u32[]{:S(2)}) copy-start(bf16[128,8,128]{2,1,0:T(8,128)(2,1)S(1)} %collective-permute-done.23.refs_1_) | copy-start | bytes 786436
  175.3 21.8 %collective-permute-start.28 = (bf16[128,8,128]{2,1,0:T(8,128)(2,1)S(1)}, bf16[128,8,128]{2,1,0:T(8,128)(2,1)S(1)}, u32[]{:S(2)}, u32[]{:S(2)}) collective-permute-start(bf16[128,8,128]{2,1,0:T(8,128)(2,1)S(1)} %copy-done.33), channel_id=1, source_target_pairs={{0,3},{1,0},{2,1},{3,2},{4,7},{5,4},{6,5},{7,6},{8,11},{9,8},{10,9... | collective-permute-start | bytes 786440 | tf_op jit(solution)/shard_map/ppermute | solution.py:191
  178.5 21.3 %copy-start.17 = (bf16[128,8,128]{2,1,0:T(8,128)(2,1)}, bf16[128,8,128]{2,1,0:T(8,128)(2,1)S(1)}, u32[]{:S(2)}) copy-start(bf16[128,8,128]{2,1,0:T(8,128)(2,1)S(1)} %collective-permute-done.24.refs_2_) | copy-start | bytes 786436
  178.5 20.5 %collective-permute-start.29 = (bf16[128,8,128]{2,1,0:T(8,128)(2,1)S(1)}, bf16[128,8,128]{2,1,0:T(8,128)(2,1)S(1)}, u32[]{:S(2)}, u32[]{:S(2)}) collective-permute-start(bf16[128,8,128]{2,1,0:T(8,128)(2,1)S(1)} %copy-done.32), channel_id=1, source_target_pairs={{0,7},{1,4},{2,5},{3,6},{4,3},{5,0},{6,1},{7,2},{8,15},{9,12},{10,... | collective-permute-start | bytes 786440 | tf_op jit(solution)/shard_map/ppermute | solution.py:191
  206.8 14.3 %collective-permute-start.30 = (f32[8,5,8,128]{3,2,1,0:T(8,128)S(1)}, f32[8,5,8,128]{3,2,1,0:T(8,128)S(1)}, u32[]{:S(2)}, u32[]{:S(2)}) collective-permute-start(f32[8,5,8,128]{3,2,1,0:T(8,128)S(1)} %constant_dynamic-slice_fusion), channel_id=1, source_target_pairs={{0,8},{8,16},{16,24},{24,32},{32,40},{40,48},{48,56},{56,64},{64,7... | collective-permute-start | bytes 491528 | tf_op jit(solution)/shard_map/ppermute | solution.py:148
  221.2 10.8 %collective-permute-start = (f32[8,5,8,128]{3,2,1,0:T(8,128)S(1)}, f32[8,5,8,128]{3,2,1,0:T(8,128)S(1)}, u32[]{:S(2)}, u32[]{:S(2)}) collective-permute-start(f32[8,5,8,128]{3,2,1,0:T(8,128)S(1)} %get-tuple-element.264), channel_id=1, source_target_pairs={{0,8},{8,16},{16,24},{24,32},{32,40},{40,48},{48,56},{56,64},{64,7... | collective-permute-start | bytes 491528 | tf_op jit(solution)/shard_map/while/body/eval_jaxpr/ppermute | solution.py:148
  221.3 10.7 %collective-permute-start.1 = (f32[8,5,8,128]{3,2,1,0:T(8,128)S(1)}, f32[8,5,8,128]{3,2,1,0:T(8,128)S(1)}, u32[]{:S(2)}, u32[]{:S(2)}) collective-permute-start(f32[8,5,8,128]{3,2,1,0:T(8,128)S(1)} %get-tuple-element.265), channel_id=1, source_target_pairs={{0,120},{8,0},{16,8},{24,16},{32,24},{40,32},{48,40},{56,48},{64,5... | collective-permute-start | bytes 491528 | tf_op jit(solution)/shard_map/while/body/eval_jaxpr/ppermute | solution.py:148
  232.0 10.3 %collective-permute-start = (f32[8,5,8,128]{3,2,1,0:T(8,128)S(1)}, f32[8,5,8,128]{3,2,1,0:T(8,128)S(1)}, u32[]{:S(2)}, u32[]{:S(2)}) collective-permute-start(f32[8,5,8,128]{3,2,1,0:T(8,128)S(1)} %get-tuple-element.264), channel_id=1, source_target_pairs={{0,8},{8,16},{16,24},{24,32},{32,40},{40,48},{48,56},{56,64},{64,7... | collective-permute-start | bytes 491528 | tf_op jit(solution)/shard_map/while/body/eval_jaxpr/ppermute | solution.py:148
  232.2 10.2 %collective-permute-start.1 = (f32[8,5,8,128]{3,2,1,0:T(8,128)S(1)}, f32[8,5,8,128]{3,2,1,0:T(8,128)S(1)}, u32[]{:S(2)}, u32[]{:S(2)}) collective-permute-start(f32[8,5,8,128]{3,2,1,0:T(8,128)S(1)} %get-tuple-element.265), channel_id=1, source_target_pairs={{0,120},{8,0},{16,8},{24,16},{32,24},{40,32},{48,40},{56,48},{64,5... | collective-permute-start | bytes 491528 | tf_op jit(solution)/shard_map/while/body/eval_jaxpr/ppermute | solution.py:148
  242.4 9.2 %collective-permute-start = (f32[8,5,8,128]{3,2,1,0:T(8,128)S(1)}, f32[8,5,8,128]{3,2,1,0:T(8,128)S(1)}, u32[]{:S(2)}, u32[]{:S(2)}) collective-permute-start(f32[8,5,8,128]{3,2,1,0:T(8,128)S(1)} %get-tuple-element.264), channel_id=1, source_target_pairs={{0,8},{8,16},{16,24},{24,32},{32,40},{40,48},{48,56},{56,64},{64,7... | collective-permute-start | bytes 491528 | tf_op jit(solution)/shard_map/while/body/eval_jaxpr/ppermute | solution.py:148
  242.6 9.3 %collective-permute-start.1 = (f32[8,5,8,128]{3,2,1,0:T(8,128)S(1)}, f32[8,5,8,128]{3,2,1,0:T(8,128)S(1)}, u32[]{:S(2)}, u32[]{:S(2)}) collective-permute-start(f32[8,5,8,128]{3,2,1,0:T(8,128)S(1)} %get-tuple-element.265), channel_id=1, source_target_pairs={{0,120},{8,0},{16,8},{24,16},{32,24},{40,32},{48,40},{56,48},{64,5... | collective-permute-start | bytes 491528 | tf_op jit(solution)/shard_map/while/body/eval_jaxpr/ppermute | solution.py:148
  251.9 5.9 %collective-permute-start = (f32[8,5,8,128]{3,2,1,0:T(8,128)S(1)}, f32[8,5,8,128]{3,2,1,0:T(8,128)S(1)}, u32[]{:S(2)}, u32[]{:S(2)}) collective-permute-start(f32[8,5,8,128]{3,2,1,0:T(8,128)S(1)} %get-tuple-element.264), channel_id=1, source_target_pairs={{0,8},{8,16},{16,24},{24,32},{32,40},{40,48},{48,56},{56,64},{64,7... | collective-permute-start | bytes 491528 | tf_op jit(solution)/shard_map/while/body/eval_jaxpr/ppermute | solution.py:148
  252.0 5.7 %collective-permute-start.1 = (f32[8,5,8,128]{3,2,1,0:T(8,128)S(1)}, f32[8,5,8,128]{3,2,1,0:T(8,128)S(1)}, u32[]{:S(2)}, u32[]{:S(2)}) collective-permute-start(f32[8,5,8,128]{3,2,1,0:T(8,128)S(1)} %get-tuple-element.265), channel_id=1, source_target_pairs={{0,120},{8,0},{16,8},{24,16},{32,24},{40,32},{48,40},{56,48},{64,5... | collective-permute-start | bytes 491528 | tf_op jit(solution)/shard_map/while/body/eval_jaxpr/ppermute | solution.py:148
  257.8 5.5 %collective-permute-start = (f32[8,5,8,128]{3,2,1,0:T(8,128)S(1)}, f32[8,5,8,128]{3,2,1,0:T(8,128)S(1)}, u32[]{:S(2)}, u32[]{:S(2)}) collective-permute-start(f32[8,5,8,128]{3,2,1,0:T(8,128)S(1)} %get-tuple-element.264), channel_id=1, source_target_pairs={{0,8},{8,16},{16,24},{24,32},{32,40},{40,48},{48,56},{56,64},{64,7... | collective-permute-start | bytes 491528 | tf_op jit(solution)/shard_map/while/body/eval_jaxpr/ppermute | solution.py:148
  258.6 4.7 %collective-permute-start.1 = (f32[8,5,8,128]{3,2,1,0:T(8,128)S(1)}, f32[8,5,8,128]{3,2,1,0:T(8,128)S(1)}, u32[]{:S(2)}, u32[]{:S(2)}) collective-permute-start(f32[8,5,8,128]{3,2,1,0:T(8,128)S(1)} %get-tuple-element.265), channel_id=1, source_target_pairs={{0,120},{8,0},{16,8},{24,16},{32,24},{40,32},{48,40},{56,48},{64,5... | collective-permute-start | bytes 491528 | tf_op jit(solution)/shard_map/while/body/eval_jaxpr/ppermute | solution.py:148
  263.4 5.5 %collective-permute-start = (f32[8,5,8,128]{3,2,1,0:T(8,128)S(1)}, f32[8,5,8,128]{3,2,1,0:T(8,128)S(1)}, u32[]{:S(2)}, u32[]{:S(2)}) collective-permute-start(f32[8,5,8,128]{3,2,1,0:T(8,128)S(1)} %get-tuple-element.264), channel_id=1, source_target_pairs={{0,8},{8,16},{16,24},{24,32},{32,40},{40,48},{48,56},{56,64},{64,7... | collective-permute-start | bytes 491528 | tf_op jit(solution)/shard_map/while/body/eval_jaxpr/ppermute | solution.py:148
  263.5 5.4 %collective-permute-start.1 = (f32[8,5,8,128]{3,2,1,0:T(8,128)S(1)}, f32[8,5,8,128]{3,2,1,0:T(8,128)S(1)}, u32[]{:S(2)}, u32[]{:S(2)}) collective-permute-start(f32[8,5,8,128]{3,2,1,0:T(8,128)S(1)} %get-tuple-element.265), channel_id=1, source_target_pairs={{0,120},{8,0},{16,8},{24,16},{32,24},{40,32},{48,40},{56,48},{64,5... | collective-permute-start | bytes 491528 | tf_op jit(solution)/shard_map/while/body/eval_jaxpr/ppermute | solution.py:148
  268.9 6.1 %collective-permute-start = (f32[8,5,8,128]{3,2,1,0:T(8,128)S(1)}, f32[8,5,8,128]{3,2,1,0:T(8,128)S(1)}, u32[]{:S(2)}, u32[]{:S(2)}) collective-permute-start(f32[8,5,8,128]{3,2,1,0:T(8,128)S(1)} %get-tuple-element.264), channel_id=1, source_target_pairs={{0,8},{8,16},{16,24},{24,32},{32,40},{40,48},{48,56},{56,64},{64,7... | collective-permute-start | bytes 491528 | tf_op jit(solution)/shard_map/while/body/eval_jaxpr/ppermute | solution.py:148
  269.1 6.0 %collective-permute-start.1 = (f32[8,5,8,128]{3,2,1,0:T(8,128)S(1)}, f32[8,5,8,128]{3,2,1,0:T(8,128)S(1)}, u32[]{:S(2)}, u32[]{:S(2)}) collective-permute-start(f32[8,5,8,128]{3,2,1,0:T(8,128)S(1)} %get-tuple-element.265), channel_id=1, source_target_pairs={{0,120},{8,0},{16,8},{24,16},{32,24},{40,32},{48,40},{56,48},{64,5... | collective-permute-start | bytes 491528 | tf_op jit(solution)/shard_map/while/body/eval_jaxpr/ppermute | solution.py:148
  279.0 8.3 %collective-permute-start.31 = (f32[4,4,16,256]{3,2,1,0:T(8,128)S(1)}, f32[4,4,16,256]{3,2,1,0:T(8,128)S(1)}, u32[]{:S(2)}, u32[]{:S(2)}) collective-permute-start(f32[4,4,16,256]{3,2,1,0:T(8,128)S(1)} %dynamic-slice_bitcast_fusion), channel_id=1, source_target_pairs={{0,4},{4,0},{1,5},{5,1},{2,6},{6,2},{3,7},{7,3},{8,12},{12,8},{9,1... | collective-permute-start | bytes 786440 | tf_op jit(solution)/shard_map/ppermute | solution.py:240
  (21 other events, 107.0 us)
Sparse Core Ops, SparseCore 0:
  94.8 62.4 reduce-scatter.2
  169.1 83.3 reduce-scatter.4
